TPU v7x, 16 devices: a whole 2x2x2 slice. The times are simulated.
16 devices in a mesh: dap: 2 (over z), dp: 8 (over y, x, core).
Axes of the slice: x: 2, y: 2, z: 2, core: 2. Of those that a mesh axis runs over, the one named last changes fastest.
Arguments:
- pair_z: bfloat16 [24, 64, 64, 128], P('dp', 'dap')
- single_s: bfloat16 [24, 64, 384], P('dp', 'dap')
- token_mask: int32 [24, 64], P('dp')
- dz_out: bfloat16 [24, 64, 64, 128], P('dp', 'dap')
- ds_out: bfloat16 [24, 64, 384], P('dp', 'dap')
- w_pa: bfloat16 [128, 512], replicated
- w_pb: bfloat16 [128, 512], replicated
- w_po: bfloat16 [512, 128], replicated
- w_bias: bfloat16 [128, 16], replicated
- w_q: bfloat16 [384, 384], replicated
- q_bias: bfloat16 [384], replicated
- w_kv: bfloat16 [384, 768], replicated
- w_g: bfloat16 [384, 384], replicated
- w_o: bfloat16 [384, 384], replicated
- w_sa: bfloat16 [384, 1536], replicated
- w_sb: bfloat16 [384, 1536], replicated
- w_so: bfloat16 [1536, 384], replicated
Outputs:
- output 1: bfloat16 [24, 64, 64, 128], P('dp', 'dap')
- output 2: bfloat16 [24, 64, 384], P('dp', 'dap')
- output 3: float32 [128, 512], replicated
- output 4: float32 [128, 512], replicated
- output 5: float32 [512, 128], replicated
- output 6: float32 [128, 16], replicated
- output 7: float32 [384, 384], replicated
- output 8: float32 [384], replicated
- output 9: float32 [384, 768], replicated
- output 10: float32 [384, 384], replicated
- output 11: float32 [384, 384], replicated
- output 12: float32 [384, 1536], replicated
- output 13: float32 [384, 1536], replicated
- output 14: float32 [1536, 384], replicated
All inputs are finite; a program needn't handle non-finite values.
Results may differ from a plain program's by a relative error of at most 0.0171153.
Values are sent between devices in bfloat16 or wider.
A program may use at most 1 GiB of HBM per device.

v0:
```python
import math
import jax
import jax.numpy as jnp
from jax import lax
from jax.sharding import PartitionSpec as P

HEAD_DIM = 24
EPSILON = 1e-5
MASK_BIG = 1e9


def contract(equation, left_op, right_op):
    return jnp.einsum(equation, left_op, right_op, preferred_element_type=jnp.float32)


def layer_norm(values):
    wide_vals = values.astype(jnp.float32)
    centred = wide_vals - jnp.mean(wide_vals, axis=-1, keepdims=True)
    inv_std = lax.rsqrt(jnp.mean(centred * centred, axis=-1, keepdims=True) + EPSILON)
    return centred * inv_std, inv_std


def norm_grad(normed, inv_std, grad_out):
    mean_grad = jnp.mean(grad_out, axis=-1, keepdims=True)
    mean_proj = jnp.mean(grad_out * normed, axis=-1, keepdims=True)
    return inv_std * (grad_out - mean_grad - normed * mean_proj)


def swiglu_grad(hid_a, hid_b, grad_hidden):
    sig_a = jax.nn.sigmoid(hid_a)
    grad_a = grad_hidden * hid_b * sig_a * (1.0 + hid_a * (1.0 - sig_a))
    return grad_a, grad_hidden * hid_a * sig_a


def pair_forward(z_rows, w_pa, w_pb, w_po, w_bias):
    normed, _ = layer_norm(z_rows)
    normed_bf = normed.astype(jnp.bfloat16)
    hid_a = contract('rjc,cf->rjf', normed_bf, w_pa)
    hid_b = contract('rjc,cf->rjf', normed_bf, w_pb)
    hidden = (jax.nn.silu(hid_a) * hid_b).astype(jnp.bfloat16)
    z_new = (z_rows.astype(jnp.float32) + contract('rjf,fc->rjc', hidden, w_po)).astype(jnp.bfloat16)
    bias_norm, _ = layer_norm(z_new)
    return z_new, contract('rjc,ch->rjh', bias_norm.astype(jnp.bfloat16), w_bias)


def pair_backward(z_rows, new_rows, dz_rows, bias_grad, w_pa, w_pb, w_po, w_bias):
    bias_norm, bias_inv = layer_norm(new_rows)
    d_w_bias = contract('rjc,rjh->ch', bias_norm.astype(jnp.bfloat16), bias_grad)
    grad_norm = contract('rjh,ch->rjc', bias_grad, w_bias)
    grad_new = dz_rows.astype(jnp.float32) + norm_grad(bias_norm, bias_inv, grad_norm)
    grad_new_bf = grad_new.astype(jnp.bfloat16)
    normed, inv_std = layer_norm(z_rows)
    normed_bf = normed.astype(jnp.bfloat16)
    hid_a = contract('rjc,cf->rjf', normed_bf, w_pa)
    hid_b = contract('rjc,cf->rjf', normed_bf, w_pb)
    hidden = (jax.nn.silu(hid_a) * hid_b).astype(jnp.bfloat16)
    d_w_po = contract('rjf,rjc->fc', hidden, grad_new_bf)
    grad_hidden = contract('rjc,fc->rjf', grad_new_bf, w_po)
    grad_a, grad_b = swiglu_grad(hid_a, hid_b, grad_hidden)
    grad_a = grad_a.astype(jnp.bfloat16)
    grad_b = grad_b.astype(jnp.bfloat16)
    d_w_pa = contract('rjc,rjf->cf', normed_bf, grad_a)
    d_w_pb = contract('rjc,rjf->cf', normed_bf, grad_b)
    grad_normed = contract('rjf,cf->rjc', grad_a, w_pa) + contract('rjf,cf->rjc', grad_b, w_pb)
    dz_in = (grad_new + norm_grad(normed, inv_std, grad_normed)).astype(jnp.bfloat16)
    return dz_in, (d_w_pa, d_w_pb, d_w_po, d_w_bias)


def solution(mesh):
    pair_spec = P('dp', 'dap', None, None)
    single_spec = P('dp', 'dap', None)

    def body(pair_z, single_s, token_mask, dz_out, ds_out, w_pa, w_pb, w_po, w_bias, w_q, q_bias, w_kv, w_g, w_o, w_sa, w_sb, w_so):
        num_cplx, num_rows, num_tok, pair_dim = pair_z.shape
        attn_width = w_q.shape[1]
        num_heads = attn_width // HEAD_DIM
        row_group = math.gcd(num_rows, 16)
        num_blocks = num_cplx * num_rows // row_group
        logit_scale = HEAD_DIM ** -0.5
        z_blocks = pair_z.reshape(num_blocks, row_group, num_tok, pair_dim)

        def forward_rows(z_rows):
            return pair_forward(z_rows, w_pa, w_pb, w_po, w_bias)

        z_new, bias_rows = lax.map(forward_rows, z_blocks)
        pair_bias = jnp.transpose(bias_rows.reshape(num_cplx, num_rows, num_tok, num_heads), (0, 3, 1, 2))

        s_norm, s_inv = layer_norm(single_s)
        act_norm = s_norm.astype(jnp.bfloat16)
        queries = (contract('bic,ce->bie', act_norm, w_q) + q_bias.astype(jnp.float32)).astype(jnp.bfloat16)
        kv_local = contract('bic,ce->bie', act_norm, w_kv).astype(jnp.bfloat16)
        gate_vals = jax.nn.sigmoid(contract('bic,ce->bie', act_norm, w_g))
        kv_all = lax.all_gather(kv_local, 'dap', axis=1, tiled=True)
        key_heads = kv_all[:, :, :attn_width].reshape(num_cplx, num_tok, num_heads, HEAD_DIM)
        value_heads = kv_all[:, :, attn_width:].reshape(num_cplx, num_tok, num_heads, HEAD_DIM)
        query_heads = queries.reshape(num_cplx, num_rows, num_heads, HEAD_DIM)
        key_mask = MASK_BIG * (token_mask.astype(jnp.float32) - 1.0)
        logits = contract('bihd,bjhd->bhij', query_heads, key_heads) * logit_scale + pair_bias + key_mask[:, None, None, :]
        attn_prob = jax.nn.softmax(logits, axis=-1)
        prob_bf = attn_prob.astype(jnp.bfloat16)
        attended = contract('bhij,bjhd->bihd', prob_bf, value_heads).reshape(num_cplx, num_rows, attn_width)
        gated = (gate_vals * attended).astype(jnp.bfloat16)
        s_mid = (single_s.astype(jnp.float32) + contract('bie,ec->bic', gated, w_o)).astype(jnp.bfloat16)
        mid_norm, mid_inv = layer_norm(s_mid)
        mid_act = mid_norm.astype(jnp.bfloat16)
        trans_a = contract('bic,cf->bif', mid_act, w_sa)
        trans_b = contract('bic,cf->bif', mid_act, w_sb)
        trans_hidden = (jax.nn.silu(trans_a) * trans_b).astype(jnp.bfloat16)

        d_w_so = contract('bif,bic->fc', trans_hidden, ds_out)
        grad_hidden = contract('bic,fc->bif', ds_out, w_so)
        grad_ta, grad_tb = swiglu_grad(trans_a, trans_b, grad_hidden)
        grad_ta = grad_ta.astype(jnp.bfloat16)
        grad_tb = grad_tb.astype(jnp.bfloat16)
        d_w_sa = contract('bic,bif->cf', mid_act, grad_ta)
        d_w_sb = contract('bic,bif->cf', mid_act, grad_tb)
        grad_mid_norm = contract('bif,cf->bic', grad_ta, w_sa) + contract('bif,cf->bic', grad_tb, w_sb)
        grad_mid = ds_out.astype(jnp.float32) + norm_grad(mid_norm, mid_inv, grad_mid_norm)
        grad_mid_bf = grad_mid.astype(jnp.bfloat16)
        d_w_o = contract('bie,bic->ec', gated, grad_mid_bf)
        grad_gated = contract('bic,ec->bie', grad_mid_bf, w_o)
        grad_gate_pre = (grad_gated * attended * gate_vals * (1.0 - gate_vals)).astype(jnp.bfloat16)
        grad_att = (grad_gated * gate_vals).astype(jnp.bfloat16).reshape(num_cplx, num_rows, num_heads, HEAD_DIM)
        grad_prob = contract('bihd,bjhd->bhij', grad_att, value_heads)
        grad_values = contract('bhij,bihd->bjhd', prob_bf, grad_att)
        grad_logits = attn_prob * (grad_prob - jnp.sum(attn_prob * grad_prob, axis=-1, keepdims=True))
        grad_logits_bf = grad_logits.astype(jnp.bfloat16)
        grad_query = contract('bhij,bjhd->bihd', grad_logits_bf, key_heads) * logit_scale
        grad_keys = contract('bhij,bihd->bjhd', grad_logits_bf, query_heads) * logit_scale
        grad_kv_part = jnp.concatenate([grad_keys.reshape(num_cplx, num_tok, attn_width), grad_values.reshape(num_cplx, num_tok, attn_width)], axis=-1).astype(jnp.bfloat16)
        grad_kv = lax.psum_scatter(grad_kv_part, 'dap', scatter_dimension=1, tiled=True)
        grad_query_bf = grad_query.reshape(num_cplx, num_rows, attn_width).astype(jnp.bfloat16)
        d_w_q = contract('bic,bie->ce', act_norm, grad_query_bf)
        d_q_bias = jnp.sum(grad_query, axis=(0, 1)).reshape(attn_width)
        d_w_kv = contract('bic,bie->ce', act_norm, grad_kv)
        d_w_g = contract('bic,bie->ce', act_norm, grad_gate_pre)
        grad_act = contract('bie,ce->bic', grad_query_bf, w_q) + contract('bie,ce->bic', grad_kv, w_kv) + contract('bie,ce->bic', grad_gate_pre, w_g)
        ds_in = (grad_mid + norm_grad(s_norm, s_inv, grad_act)).astype(jnp.bfloat16)

        grad_bias = jnp.transpose(grad_logits_bf, (0, 2, 3, 1)).reshape(num_blocks, row_group, num_tok, num_heads)
        dz_blocks = dz_out.reshape(num_blocks, row_group, num_tok, pair_dim)

        def backward_rows(running, block_in):
            z_rows, new_rows, dz_rows, bias_grad = block_in
            dz_rows_in, row_grads = pair_backward(z_rows, new_rows, dz_rows, bias_grad, w_pa, w_pb, w_po, w_bias)
            return tuple(acc_sum + update for acc_sum, update in zip(running, row_grads)), dz_rows_in

        zero_grads = (jnp.zeros(w_pa.shape, jnp.float32), jnp.zeros(w_pb.shape, jnp.float32), jnp.zeros(w_po.shape, jnp.float32), jnp.zeros(w_bias.shape, jnp.float32))
        pair_grads, dz_in = lax.scan(backward_rows, zero_grads, (z_blocks, z_new, dz_blocks, grad_bias))
        weight_grads = lax.psum(pair_grads + (d_w_q, d_q_bias, d_w_kv, d_w_g, d_w_o, d_w_sa, d_w_sb, d_w_so), ('dap', 'dp'))
        return (dz_in.reshape(num_cplx, num_rows, num_tok, pair_dim), ds_in) + weight_grads

    in_specs = (pair_spec, single_spec, P('dp', None), pair_spec, single_spec) + (P(),) * 12
    out_specs = (pair_spec, single_spec) + (P(),) * 12
    return jax.shard_map(body, mesh=mesh, in_specs=in_specs, out_specs=out_specs, check_vma=False)
```

profile of v0, /device:TPU:0, one launch (start us, length us, event | category | flops | bytes accessed | tf_op | source)
XLA Modules:
  0.0 376.1 jit_solution(1328187765898118169)
XLA Ops:
  12.2 7.8 %all_gather.3 = bf16[3,64,768]{2,1,0:T(8,128)(2,1)S(1)} all-gather(bf16[3,32,768]{2,1,0:T(8,128)(2,1)S(1)} %convolution_convert_fusion.1), channel_id=1, replica_groups=mesh['dap'=2,'dp'=8] {'dap'}, dimensions={1}, use_global_device_ids=true | all-gather | bytes 442368 | tf_op jit(solution)/shard_map/all_gather | solution.py:93
  25.6 45.1 %while.31 = (s32[]{:T(128)}, bf16[6,16,64,128]{3,2,1,0:T(8,128)(2,1)}, f32[6,16,64,16]{2,3,1,0:T(8,128)}, bf16[6,16,64,128]{3,2,1,0:T(8,128)(2,1)S(1)}, bf16[128...) while((s32[]{:T(128)}, ...), condition=%wide.region_5.6_spmd, body=%wide.region_0.5_spmd.sunk | while | flops 413534208 | bytes 7443573 | solution.py:85
  26.3 1.8 fusion.252
  28.1 3.3 bitcast_dynamic-update-slice_fusion.2
  35.6 3.3 bitcast_dynamic-update-slice_fusion.2
  43.1 3.3 bitcast_dynamic-update-slice_fusion.2
  50.6 3.3 bitcast_dynamic-update-slice_fusion.2
  56.3 1.8 fusion.252
  58.1 3.3 bitcast_dynamic-update-slice_fusion.2
  65.7 3.3 bitcast_dynamic-update-slice_fusion.2
  70.7 2.8 fusion.167
  84.7 2.4 convolution_convert_fusion
  89.5 1.8 multiply_convert_fusion.5
  91.3 2.0 fusion.97
  95.6 2.7 fusion.173
  98.3 2.0 convolution_bitcast_fusion.9
  103.7 96.4 %while.32 = (s32[]{:T(128)}, f32[128,512]{1,0:T(8,128)S(1)}, f32[128,512]{1,0:T(8,128)S(1)}, f32[512,128]{1,0:T(8,128)}, f32[128,16]{0,1:T(8,128)}, /*index=5*/b...) while((s32[]{:T(128)}, f32[128,512]{1,0:T(8,128)S(1)}, ...), condition=%wide.region_24.25_spmd.clone, body=%wide.region_15.24_spmd.clone.sunk | while | flops 1101010944 | bytes 33282852 | solution.py:149
  106.4 2.1 fusion.278
  122.5 2.1 fusion.278
  138.5 2.1 fusion.278
  154.6 2.1 fusion.278
  170.7 2.1 fusion.278
  186.7 2.1 fusion.278
  200.1 2.5 convolution_bitcast_fusion.11
  202.6 2.1 convolution_bitcast_fusion.10
  204.7 1.9 convolution_bitcast_fusion.6
  206.7 1.9 convolution_bitcast_fusion.7
  208.6 1.9 convolution_bitcast_fusion.5
  210.5 2.3 convolution_bitcast_fusion.8
  213.6 34.2 %all-reduce = (f32[128,16]{0,1:T(8,128)}, f32[384]{0:T(512)}) all-reduce(f32[128,16]{0,1:T(8,128)} %get-tuple-element.139, f32[384]{0:T(512)S(1)} %reshape.197), channel_id=1, replica_groups=mesh['dap'=2,'dp'=8] {'dap','dp'}, use_global_device_ids=true, to_apply=%region_31.32 | all-reduce | flops 2432 | bytes 19456 | tf_op jit(solution)/shard_map/psum | solution.py:150
  249.6 103.5 %all-reduce.4.cloned.1.call-done = (f32[128,512]{1,0:T(8,128)}, f32[128,512]{1,0:T(8,128)}, f32[512,128]{1,0:T(8,128)}, f32[384,384]{1,0:T(8,128)}, f32[384,768]...) async-done(((f32[128,512]{1,0:T(8,128)}, f32[128,512]{1,0:T(8,128)}, ...) | async-done | bytes 10813456 | tf_op jit(solution)/shard_map/psum | solution.py:150
  358.2 2.0 copy.109
  (402 shorter events, 150.6 us)
Async XLA Ops:
  7.2 73.3 %copy-start = (bf16[1536,384]{1,0:T(8,128)(2,1)S(1)}, bf16[1536,384]{1,0:T(8,128)(2,1)}, u32[]{:S(2)}) copy-start(bf16[1536,384]{1,0:T(8,128)(2,1)} %param.37) | copy-start | bytes 3538948
  7.2 13.8 %copy-start.7 = (bf16[3,32,384]{2,1,0:T(8,128)(2,1)S(1)}, bf16[3,32,384]{2,1,0:T(8,128)(2,1)}, u32[]{:S(2)}) copy-start(bf16[3,32,384]{2,1,0:T(8,128)(2,1)} %param.22) | copy-start | bytes 221188
  7.2 203.3 %reduce-scatter.2.cloned.1.call-start = ((), (), s32[]{:S(2)}) async-start(), calls=%async_computation.1 | async-start | bytes 442368 | tf_op jit(solution)/shard_map/reduce_scatter | solution.py:131
  20.0 5.6 %copy-start.2 = (bf16[3,32,64,128]{3,2,1,0:T(8,128)(2,1)S(1)}, bf16[3,32,64,128]{3,2,1,0:T(8,128)(2,1)}, u32[]{:S(2)}) copy-start(bf16[3,32,64,128]{3,2,1,0:T(8,128)(2,1)} %param.21) | copy-start | bytes 4718596
  20.1 5.5 %copy-start.3 = (bf16[128,512]{1,0:T(8,128)(2,1)S(1)}, bf16[128,512]{1,0:T(8,128)(2,1)}, u32[]{:S(2)}) copy-start(bf16[128,512]{1,0:T(8,128)(2,1)} %param.27) | copy-start | bytes 393220
  20.1 5.5 %copy-start.4 = (bf16[128,512]{1,0:T(8,128)(2,1)S(1)}, bf16[128,512]{1,0:T(8,128)(2,1)}, u32[]{:S(2)}) copy-start(bf16[128,512]{1,0:T(8,128)(2,1)} %param.26) | copy-start | bytes 393220
  20.1 5.5 %copy-start.51 = (bf16[128,16]{0,1:T(8,128)(2,1)S(1)}, bf16[128,16]{0,1:T(8,128)(2,1)}, u32[]{:S(2)}) copy-start(bf16[128,16]{0,1:T(8,128)(2,1)} %param.29) | copy-start | bytes 12292
  21.0 4.6 %copy-start.57 = (bf16[512,128]{1,0:T(8,128)(2,1)S(1)}, bf16[512,128]{1,0:T(8,128)(2,1)}, u32[]{:S(2)}) copy-start(bf16[512,128]{1,0:T(8,128)(2,1)} %param.28) | copy-start | bytes 393220
  73.5 16.0 %copy-start.40 = (f32[3,16,32]{2,1,0:T(8,128)}, f32[3,16,32]{2,1,0:T(8,128)S(1)}, u32[]{:S(2)}) copy-start(f32[3,16,32]{2,1,0:T(8,128)S(1)} %get-tuple-element.249) | copy-start | bytes 18436
  74.0 15.5 %copy-start.49 = (f32[3,16,32]{2,1,0:T(8,128)}, f32[3,16,32]{2,1,0:T(8,128)S(1)}, u32[]{:S(2)}) copy-start(f32[3,16,32]{2,1,0:T(8,128)S(1)} %fusion.125) | copy-start | bytes 18436
  82.8 4.3 %copy-start.17 = (f32[3,32,384]{2,1,0:T(8,128)}, f32[3,32,384]{2,1,0:T(8,128)S(1)}, u32[]{:S(2)}) copy-start(f32[3,32,384]{2,1,0:T(8,128)S(1)} %multiply_add_fusion) | copy-start | bytes 442372
  88.3 5.0 %copy-start.52 = (f32[3,16,32]{2,1,0:T(8,128)}, f32[3,16,32]{2,1,0:T(8,128)S(1)}, u32[]{:S(2)}) copy-start(f32[3,16,32]{2,1,0:T(8,128)S(1)} %get-tuple-element.273) | copy-start | bytes 18436
  93.3 7.1 %copy-start.13 = (f32[3,16,32,64]{3,2,1,0:T(8,128)S(1)}, f32[3,16,32,64]{3,2,1,0:T(8,128)}, u32[]{:S(2)}) copy-start(f32[3,16,32,64]{3,2,1,0:T(8,128)} %get-tuple-element.267) | copy-start | bytes 1179652
  95.3 257.8 %all-reduce.4.cloned.1.call-start = ((), (), s32[]{:S(2)}) async-start(), calls=%async_computation.2 | async-start | bytes 21626880 | tf_op jit(solution)/shard_map/psum | solution.py:150
  95.5 4.8 %copy-start.14 = (f32[3,16,32,64]{3,2,1,0:T(8,128)S(1)}, f32[3,16,32,64]{3,2,1,0:T(8,128)}, u32[]{:S(2)}) copy-start(f32[3,16,32,64]{3,2,1,0:T(8,128)} %get-tuple-element.274) | copy-start | bytes 1179652
  95.6 4.8 %copy-start.15 = (f32[6,16,64,16]{2,3,1,0:T(8,128)S(1)}, f32[6,16,64,16]{2,3,1,0:T(8,128)}, u32[]{:S(2)}) copy-start(f32[6,16,64,16]{2,3,1,0:T(8,128)} %get-tuple-element.134) | copy-start | bytes 1179652
  95.6 4.8 %copy-start.41 = (f32[3,16,32]{2,1,0:T(8,128)S(1)}, f32[3,16,32]{2,1,0:T(8,128)}, u32[]{:S(2)}) copy-start(f32[3,16,32]{2,1,0:T(8,128)} %copy-done.40) | copy-start | bytes 18436
  95.6 4.8 %copy-start.50 = (f32[3,16,32]{2,1,0:T(8,128)S(1)}, f32[3,16,32]{2,1,0:T(8,128)}, u32[]{:S(2)}) copy-start(f32[3,16,32]{2,1,0:T(8,128)} %copy-done.49) | copy-start | bytes 18436
  95.6 4.8 %copy-start.53 = (f32[3,16,32]{2,1,0:T(8,128)S(1)}, f32[3,16,32]{2,1,0:T(8,128)}, u32[]{:S(2)}) copy-start(f32[3,16,32]{2,1,0:T(8,128)} %copy-done.52) | copy-start | bytes 18436
  103.7 96.4 %copy-start.8 = (bf16[3,32,384]{2,1,0:T(8,128)(2,1)S(1)}, bf16[3,32,384]{2,1,0:T(8,128)(2,1)}, u32[]{:S(2)}) copy-start(bf16[3,32,384]{2,1,0:T(8,128)(2,1)} %param.22) | copy-start | bytes 221188
  200.1 6.5 %copy-start.5 = (f32[128,512]{1,0:T(8,128)}, f32[128,512]{1,0:T(8,128)S(1)}, u32[]{:S(2)}) copy-start(f32[128,512]{1,0:T(8,128)S(1)} %get-tuple-element.137) | copy-start | bytes 786436
  200.1 6.5 %copy-start.6 = (f32[128,512]{1,0:T(8,128)}, f32[128,512]{1,0:T(8,128)S(1)}, u32[]{:S(2)}) copy-start(f32[128,512]{1,0:T(8,128)S(1)} %get-tuple-element.136) | copy-start | bytes 786436
  200.1 4.6 %copy-start.24 = (bf16[3,32,384]{2,1,0:T(8,128)(2,1)S(1)}, bf16[3,32,384]{2,1,0:T(8,128)(2,1)}, u32[]{:S(2)}) copy-start(bf16[3,32,384]{2,1,0:T(8,128)(2,1)} %copy-done.23) | copy-start | bytes 221188
  200.1 4.6 %copy-start.31 = (bf16[3,32,1536]{2,1,0:T(8,128)(2,1)S(1)}, bf16[3,32,1536]{2,1,0:T(8,128)(2,1)}, u32[]{:S(2)}) copy-start(bf16[3,32,1536]{2,1,0:T(8,128)(2,1)} %copy-done.30) | copy-start | bytes 884740
  212.8 35.0 %copy-start.16 = (bf16[3,32,16,24]{1,3,2,0:T(8,128)(2,1)S(1)}, bf16[3,32,16,24]{1,3,2,0:T(8,128)(2,1)}, u32[]{:S(2)}) copy-start(bf16[3,32,16,24]{1,3,2,0:T(8,128)(2,1)} %get-tuple-element.262) | copy-start | bytes 221188
  212.8 35.0 %copy-start.29 = (bf16[384,384]{1,0:T(8,128)(2,1)S(1)}, bf16[384,384]{1,0:T(8,128)(2,1)}, u32[]{:S(2)}) copy-start(bf16[384,384]{1,0:T(8,128)(2,1)} %param.30) | copy-start | bytes 884740
  212.9 35.3 %copy-start.22 = (bf16[384,768]{1,0:T(8,128)(2,1)S(1)}, bf16[384,768]{1,0:T(8,128)(2,1)}, u32[]{:S(2)}) copy-start(bf16[384,768]{1,0:T(8,128)(2,1)} %param.32) | copy-start | bytes 1769476
  212.9 35.3 %copy-start.39 = (bf16[3,32,768]{2,1,0:T(8,128)(2,1)S(1)}, bf16[3,32,768]{2,1,0:T(8,128)(2,1)}, u32[]{:S(2)}) copy-start(bf16[3,32,768]{2,1,0:T(8,128)(2,1)} %reduce-scatter.2.cloned.1.call-done) | copy-start | bytes 442372
  212.9 35.6 %copy-start.32 = (bf16[3,32,384]{2,1,0:T(8,128)(2,1)S(1)}, bf16[3,32,384]{2,1,0:T(8,128)(2,1)}, u32[]{:S(2)}) copy-start(bf16[3,32,384]{2,1,0:T(8,128)(2,1)} %get-tuple-element.263) | copy-start | bytes 221188
  212.9 35.6 %copy-start.46 = (bf16[384,384]{1,0:T(8,128)(2,1)S(1)}, bf16[384,384]{1,0:T(8,128)(2,1)}, u32[]{:S(2)}) copy-start(bf16[384,384]{1,0:T(8,128)(2,1)} %param.33) | copy-start | bytes 884740
  212.9 36.0 %copy-start.18 = (f32[3,32,384]{2,1,0:T(8,128)S(1)}, f32[3,32,384]{2,1,0:T(8,128)}, u32[]{:S(2)}) copy-start(f32[3,32,384]{2,1,0:T(8,128)} %copy-done.17) | copy-start | bytes 442372
  353.1 7.1 %copy-start.26 = (f32[384,768]{1,0:T(8,128)S(1)}, f32[384,768]{1,0:T(8,128)}, u32[]{:S(2)}) copy-start(f32[384,768]{1,0:T(8,128)} %get-tuple-element.520) | copy-start | bytes 3538948
  (44 other events, 71.6 us)
Sparse Core Ops, SparseCore 0:
  95.4 11.4 reduce-scatter.1
  213.0 140.0 all-reduce.3
where the time goes:
time: 378 us; the launch traced here: 376 us
  matrix products  130 us (34%)
  waiting for transfers between devices  103 us (27%)
  other arithmetic  52.1 us (14%)
  blocking collectives  42 us (11%)
  local copies, waits for them, and re-layouts  32.1 us (8%)
  between operations  14.7 us (4%)
    dot_general x104, matrix products, contract(): jnp.einsum(equation, left_op, right_op, preferred_element_type=jnp.float32)  130 us
    psum x1, waiting for transfers between devices, body(): lax.psum(pair_grads + (d_w_q, d_q_bias, d_w_kv, d_w_g, d_w_o, d_w_sa, d_w...  103 us
    psum x1, blocking collectives, body(): lax.psum(pair_grads + (d_w_q, d_q_bias, d_w_kv, d_w_g, d_w_o, d_w_sa, d_w...  34.2 us
    unnamed x122, local copies, waits for them, and re-layouts  17.6 us
    reduce_sum x26, other arithmetic, layer_norm(): jnp.mean(centred * centred, axis=-1, keepdims=True) + EPSILON  16.3 us
    reduce_sum x19, other arithmetic, layer_norm(): centred = wide_vals - jnp.mean(wide_vals, axis=-1, keepdims=True)  11.2 us
    add x6, other arithmetic, pair_backward(): dz_rows.astype(jnp.float32) + norm_grad(bias_norm, bias_inv, grad_norm)  9.86 us
    dynamic_update_slice x6, other arithmetic, body(): z_new, bias_rows = lax.map(forward_rows, z_blocks)  7.94 us
  transfers between devices with their start and end apart: 2, of which 1 were waited for; matrix products, arithmetic and copies ran while one was open for 30% of the time, Pallas kernels for 0%

commit v1 on v0

v1 whole, which is shorter than its diff:
```python
import jax
import jax.numpy as jnp
from jax import lax
from jax.experimental import pallas as pl
from jax.experimental.pallas import tpu as pltpu
from jax.sharding import PartitionSpec as P

HEADS = 16
HEAD_DIM = 24
EPSILON = 1e-5
MASK_BIG = 1e9
BF = jnp.bfloat16
F32 = jnp.float32
ROWS_S, ROWS_A, ROWS_P = 4608, 2048, 768
LANES = 128


def nn(a, b):
    return lax.dot_general(a, b, (((1,), (0,)), ((), ())), preferred_element_type=F32)


def nt(a, b):
    return lax.dot_general(a, b, (((1,), (1,)), ((), ())), preferred_element_type=F32)


def tn(a, b):
    return lax.dot_general(a, b, (((0,), (0,)), ((), ())), preferred_element_type=F32)


def sigmoid(x):
    return 0.5 * jnp.tanh(0.5 * x) + 0.5


def layer_norm(vals):
    centred = vals - jnp.mean(vals, axis=-1, keepdims=True)
    inv = lax.rsqrt(jnp.mean(centred * centred, axis=-1, keepdims=True) + EPSILON)
    return centred * inv, inv


def norm_grad(normed, inv, grad):
    mean_grad = jnp.mean(grad, axis=-1, keepdims=True)
    mean_proj = jnp.mean(grad * normed, axis=-1, keepdims=True)
    return inv * (grad - mean_grad - normed * mean_proj)


def swiglu_grad(ha, hb, dh):
    sig = sigmoid(ha)
    silu = ha * sig
    hidden = silu * hb
    grad_a = dh * hb * (sig * (1.0 + (ha - silu)))
    return hidden.astype(BF), grad_a.astype(BF), (dh * silu).astype(BF)


class Reducer:
    def __init__(self, place, rows, grads, recvs, final, send_sem, recv_sem):
        self.place, self.rows, self.grads, self.recvs, self.final = place, rows, grads, recvs, final
        self.send_sem, self.recv_sem = send_sem, recv_sem
        coords = place["coords"]
        self.order = [("x", "y", "z"), ("y", "z", "x"), ("z", "x", "y")]
        self.base = []
        for third in range(3):
            base = [coords["core"] * (rows // 2)]
            for depth, axis in enumerate(self.order[third]):
                base.append(base[-1] + coords[axis] * (rows >> (depth + 2)))
            self.base.append(base)

    def copy(self, stage, third):
        rows, base, order = self.rows, self.base[third], self.order[third]
        coords = self.place["coords"]
        step = rows // 16
        if stage < 4:
            size = rows >> (stage + 1)
            axis = "core" if stage == 0 else order[stage - 1]
            low = 0 if stage == 0 else base[stage - 1]
            start = pl.multiple_of(low + (1 - coords[axis]) * size, step)
            src = self.grads.at[third, pl.ds(start, size)]
            dst = self.recvs[stage].at[third]
        else:
            size = rows >> (8 - stage)
            axis = "core" if stage == 7 else order[6 - stage]
            start = pl.multiple_of(base[7 - stage], step)
            src = self.final.at[third, pl.ds(start, size)]
            dst = src
        return pltpu.make_async_remote_copy(
            src_ref=src, dst_ref=dst,
            send_sem=self.send_sem.at[stage, third], recv_sem=self.recv_sem.at[stage, third],
            device_id=self.place["peers"][axis], device_id_type=pl.DeviceIdType.MESH)

    def start(self, stage):
        for third in range(3):
            self.copy(stage, third).start()

    def step(self, stage):
        for third in range(3):
            done = stage - 1
            self.copy(done, third).wait()
            if done < 4:
                size = self.rows >> (done + 1)
                chunk = self.rows // 16
                low = self.base[third][done]
                dest = self.final if done == 3 else self.grads
                recv = self.recvs[done]

                def add(k, carry):
                    at = pl.ds(pl.multiple_of(low + k * chunk, chunk), chunk)
                    off = pl.ds(pl.multiple_of(k * chunk, chunk), chunk)
                    dest[third, at, :] = (self.grads[third, at, :].astype(F32) + recv[third, off, :].astype(F32)).astype(BF)
                    return carry

                lax.fori_loop(0, size // chunk, add, 0)
            if stage < 8:
                self.copy(stage, third).start()


def body_kernel(
        z_hbm, dz_hbm, wpa_hbm, wpb_hbm, wpo_hbm, wq_hbm, wkv_hbm, wg_hbm, wo_hbm, wsa_hbm, wsb_hbm, wso_hbm,
        s_ref, ds_ref, mask_ref, qb_ref, wbias_ref,
        dzin_ref, dsin_ref, fs_ref, fa_ref, fp_ref,
        z_v, dz_v, wpa, wpb, wpo, wq, wkv, wg, wo, wsa, wsb, wso,
        z1_v, w8, bias_v, prob_v, act_v, q_v, gate_v, att_v, gated_v, gatt_v, gmid_v, kv_v, gkv_v, gkvr_v,
        dwpa, dwpb, dwpo, m8,
        gs, gs0, gs1, gs2, gs3, ga_, ga0, ga1, ga2, ga3, gp, gp0, gp1, gp2, gp3,
        in_sem, kv_sem, send_sem, recv_sem):
    dap = lax.axis_index("dap")
    dp = lax.axis_index("dp")
    core = lax.rem(dp, 2)
    cx = lax.rem(dp // 2, 2)
    cy = dp // 4
    peers = {
        "core": (dap, dp + 1 - 2 * core),
        "x": (dap, dp + 2 - 4 * cx),
        "y": (dap, dp + 4 - 8 * cy),
        "z": (1 - dap, dp),
    }
    place = {"coords": {"core": core, "x": cx, "y": cy, "z": dap}, "peers": peers}
    num_cplx, num_tok = mask_ref.shape
    half = num_tok // 2
    width = HEADS * HEAD_DIM

    loads = [(wkv_hbm, wkv), (wq_hbm, wq), (wg_hbm, wg), (wpa_hbm, wpa), (wpb_hbm, wpb), (wpo_hbm, wpo), (z_hbm, z_v),
             (wo_hbm, wo), (wsa_hbm, wsa), (wsb_hbm, wsb), (wso_hbm, wso), (dz_hbm, dz_v)]
    copies = [pltpu.make_async_copy(src, dst, in_sem.at[k]) for k, (src, dst) in enumerate(loads)]
    for item in copies:
        item.start()

    barrier = pltpu.get_barrier_semaphore()
    for peer in peers.values():
        pl.semaphore_signal(barrier, inc=1, device_id=peer, device_id_type=pl.DeviceIdType.MESH)
    pl.semaphore_wait(barrier, 4)

    red_s = Reducer(place, ROWS_S, gs, (gs0, gs1, gs2, gs3), fs_ref, send_sem.at[0], recv_sem.at[0])
    red_a = Reducer(place, ROWS_A, ga_, (ga0, ga1, ga2, ga3), fa_ref, send_sem.at[1], recv_sem.at[1])
    red_p = Reducer(place, ROWS_P, gp, (gp0, gp1, gp2, gp3), fp_ref, send_sem.at[2], recv_sem.at[2])

    s_f = s_ref[...].astype(F32)
    s_norm, s_inv = layer_norm(s_f)
    act = s_norm.astype(BF)
    act_v[...] = act
    copies[0].wait()
    kv_v[dap] = nn(act, wkv[...]).astype(BF)

    def kv_copy():
        return pltpu.make_async_remote_copy(
            src_ref=kv_v.at[dap], dst_ref=kv_v.at[dap], send_sem=kv_sem.at[0], recv_sem=kv_sem.at[1],
            device_id=peers["z"], device_id_type=pl.DeviceIdType.MESH)

    def gkv_copy():
        return pltpu.make_async_remote_copy(
            src_ref=gkv_v.at[1 - dap], dst_ref=gkvr_v, send_sem=kv_sem.at[2], recv_sem=kv_sem.at[3],
            device_id=peers["z"], device_id_type=pl.DeviceIdType.MESH)

    kv_copy().start()
    copies[1].wait()
    copies[2].wait()
    q_v[...] = (nn(act, wq[...]) + qb_ref[...].astype(F32)).astype(BF)
    gate_v[...] = sigmoid(nn(act, wg[...]))

    row_head = lax.broadcasted_iota(jnp.int32, (128, HEADS), 0)
    col_head = lax.broadcasted_iota(jnp.int32, (128, HEADS), 1)
    pick = jnp.where((row_head >= col_head * 8) & (row_head < col_head * 8 + 8), 1.0, 0.0).astype(BF)
    spread = nt(pick, wbias_ref[...])
    row8 = lax.rem(lax.broadcasted_iota(jnp.int32, (128, LANES), 0), 8)
    for k in range(8):
        w8[:, k * LANES:(k + 1) * LANES] = jnp.where(row8 == k, spread, 0.0).astype(BF)

    for k in range(3, 7):
        copies[k].wait()

    blk = 8 * num_tok
    per_cplx = half // 8
    num_blk = num_cplx * per_cplx

    def side_by_side(tokens):
        return jnp.concatenate([tokens[k * num_tok:(k + 1) * num_tok] for k in range(8)], axis=1)

    def pair_forward(b, carry):
        at = pl.ds(pl.multiple_of(b * blk, blk), blk)
        z_f = z_v[at, :].astype(F32)
        normed, _ = layer_norm(z_f)
        u = normed.astype(BF)
        total = z_f
        for f in range(0, 512, 256):
            ha = nn(u, wpa[:, f:f + 256])
            hb = nn(u, wpb[:, f:f + 256])
            hidden = (ha * sigmoid(ha) * hb).astype(BF)
            total = total + nn(hidden, wpo[f:f + 256, :])
        z1 = total.astype(BF)
        z1_v[at, :] = z1
        bias_norm, _ = layer_norm(z1.astype(F32))
        bias8 = nt(w8[...], side_by_side(bias_norm.astype(BF)))
        c, i0 = b // per_cplx, pl.multiple_of(lax.rem(b, per_cplx) * 8, 8)
        bias_v[c, :, pl.ds(i0, 8), :] = bias8.reshape(HEADS, 8, num_tok)
        return carry

    lax.fori_loop(0, num_blk, pair_forward, 0)

    scale = HEAD_DIM ** -0.5
    grow = lax.broadcasted_iota(jnp.int32, (HEADS, 1, width), 0) * HEAD_DIM
    gcol = lax.broadcasted_iota(jnp.int32, (HEADS, 1, width), 2)
    head_mask = (gcol >= grow) & (gcol < grow + HEAD_DIM)

    def expand(rows):
        wide = jnp.where(head_mask, rows.astype(F32)[None], 0.0)
        return wide.reshape(HEADS * half, width).astype(BF)

    def gather_heads(wide):
        return jnp.sum(jnp.where(head_mask, wide.reshape(HEADS, half, width), 0.0), axis=0)

    def tokens_of(c, lo):
        rows = slice(c * half, (c + 1) * half)
        return jnp.concatenate([kv_v[0, rows, lo:lo + width], kv_v[1, rows, lo:lo + width]], axis=0)

    kv_copy().wait()
    for c in range(num_cplx):
        rows = slice(c * half, (c + 1) * half)
        key_mask = MASK_BIG * (mask_ref[c:c + 1, :].astype(F32) - 1.0)
        logits = nt(expand(q_v[rows, :]), tokens_of(c, 0)) * scale + bias_v[c].reshape(HEADS * half, num_tok) + key_mask
        ex = jnp.exp(logits - jnp.max(logits, axis=-1, keepdims=True))
        prob = ex / jnp.sum(ex, axis=-1, keepdims=True)
        prob_v[c] = prob
        att_v[rows, :] = gather_heads(nn(prob.astype(BF), tokens_of(c, width)))
    gated = (gate_v[...] * att_v[...]).astype(BF)
    gated_v[...] = gated
    copies[7].wait()
    s_mid = (s_ref[...].astype(F32) + nn(gated, wo[...])).astype(BF)
    mid_norm, mid_inv = layer_norm(s_mid.astype(F32))
    mid_act = mid_norm.astype(BF)
    mid_t = mid_act.T

    for k in range(8, 11):
        copies[k].wait()
    ds_b = ds_ref[...]
    grad_mid_norm = None
    for t in range(3):
        cols = slice(t * 512, (t + 1) * 512)
        ta = nn(mid_act, wsa[:, cols])
        tb = nn(mid_act, wsb[:, cols])
        dh = nt(ds_b, wso[cols, :])
        hidden, grad_a, grad_b = swiglu_grad(ta, tb, dh)
        part = nt(grad_a, wsa[:, cols]) + nt(grad_b, wsb[:, cols])
        grad_mid_norm = part if grad_mid_norm is None else grad_mid_norm + part
        d_sa = nn(mid_t, grad_a).astype(BF)
        d_sb = nn(mid_t, grad_b).astype(BF)
        for k in range(4):
            gs[t, k * 384:(k + 1) * 384, :] = d_sa[:, k * LANES:(k + 1) * LANES]
            gs[t, 1536 + k * 384:1536 + (k + 1) * 384, :] = d_sb[:, k * LANES:(k + 1) * LANES]
        d_so = tn(hidden, ds_b).astype(BF)
        for k in range(3):
            gs[k, 3072 + t * 512:3072 + (t + 1) * 512, :] = d_so[:, k * LANES:(k + 1) * LANES]
    red_s.start(0)
    grad_mid = ds_b.astype(F32) + norm_grad(mid_norm, mid_inv, grad_mid_norm)
    gmid_v[...] = grad_mid
    grad_mid_bf = grad_mid.astype(BF)
    grad_gated = nt(grad_mid_bf, wo[...])
    gate = gate_v[...]
    gatt_v[...] = (grad_gated * gate).astype(BF)
    grad_gate_pre = (grad_gated * att_v[...] * gate * (1.0 - gate)).astype(BF)

    def put_attn(name_row, value):
        val = value.astype(BF)
        for k in range(val.shape[1] // LANES):
            per = val.shape[1] // width
            lo = name_row + (k % per) * 384
            ga_[k // per, lo:lo + 384, :] = val[:, k * LANES:(k + 1) * LANES]

    act_t = act_v[...].T
    put_attn(1152, nn(act_t, grad_gate_pre))
    put_attn(1536, tn(gated_v[...], grad_mid_bf))

    grad_q_parts = []
    for c in range(num_cplx):
        rows = slice(c * half, (c + 1) * half)
        keys, vals = tokens_of(c, 0), tokens_of(c, width)
        gatt = expand(gatt_v[rows, :])
        prob = prob_v[c]
        grad_prob = nt(gatt, vals)
        grad_vals = tn(prob.astype(BF), gatt)
        grad_logits = prob * (grad_prob - jnp.sum(prob * grad_prob, axis=-1, keepdims=True))
        bias_v[c] = grad_logits.reshape(HEADS, half, num_tok)
        gl_b = grad_logits.astype(BF)
        grad_q_parts.append(gather_heads(nn(gl_b, keys)) * scale)
        grad_keys = tn(gl_b, expand(q_v[rows, :])) * scale
        for d in range(2):
            gkv_v[d, rows, 0:width] = grad_keys[d * half:(d + 1) * half].astype(BF)
            gkv_v[d, rows, width:2 * width] = grad_vals[d * half:(d + 1) * half].astype(BF)
        if c == 1:
            red_s.step(1)
    gkv_copy().start()
    grad_q = jnp.concatenate(grad_q_parts, axis=0)
    grad_q_bf = grad_q.astype(BF)
    put_attn(0, nn(act_t, grad_q_bf))
    row16 = lax.broadcasted_iota(jnp.int32, (16, width), 0)
    bias_tile = jnp.where(row16 == 0, jnp.sum(grad_q, axis=0, keepdims=True), 0.0).astype(BF)
    for t in range(3):
        ga_[t, 1920:1936, :] = bias_tile[:, t * LANES:(t + 1) * LANES]
        ga_[t, 1936:2048, :] = jnp.zeros((112, LANES), BF)
    grad_act = nt(grad_q_bf, wq[...]) + nt(grad_gate_pre, wg[...])
    gkv_copy().wait()
    grad_kv = (gkv_v[dap].astype(F32) + gkvr_v[...].astype(F32)).astype(BF)
    put_attn(384, nn(act_t, grad_kv))
    red_a.start(0)
    grad_act = grad_act + nt(grad_kv, wkv[...])
    s_norm2, s_inv2 = layer_norm(s_ref[...].astype(F32))
    dsin_ref[...] = (gmid_v[...] + norm_grad(s_norm2, s_inv2, grad_act)).astype(BF)

    copies[11].wait()
    for ref in (dwpa, dwpb, dwpo, m8):
        ref[...] = jnp.zeros(ref.shape, F32)

    hooks = {0: [(red_a, 1)], 2: [(red_s, 2)], 3: [(red_a, 2)], 5: [(red_s, 3), (red_a, 3)], 7: [(red_s, 4), (red_a, 4)],
             9: [(red_s, 5), (red_a, 5)], 11: [(red_s, 6), (red_a, 6)]}

    def pair_backward(b, carry):
        at = pl.ds(pl.multiple_of(b * blk, blk), blk)
        c, i0 = b // per_cplx, pl.multiple_of(lax.rem(b, per_cplx) * 8, 8)
        gl = bias_v[c, :, pl.ds(i0, 8), :].reshape(8 * HEADS, num_tok).astype(BF)
        wide = tn(gl, w8[...])
        grad_norm = jnp.concatenate([wide[:, k * LANES:(k + 1) * LANES] for k in range(8)], axis=0)
        bias_norm, bias_inv = layer_norm(z1_v[at, :].astype(F32))
        m8[...] += nn(gl, side_by_side(bias_norm.astype(BF)))
        grad_new = dz_v[at, :].astype(F32) + norm_grad(bias_norm, bias_inv, grad_norm)
        gnb = grad_new.astype(BF)
        gnb_t = gnb.T
        normed, inv = layer_norm(z_v[at, :].astype(F32))
        u = normed.astype(BF)
        u_t = u.T
        grad_normed = None
        for f in range(0, 512, 256):
            cols = slice(f, f + 256)
            hidden, grad_a, grad_b = swiglu_grad(nn(u, wpa[:, cols]), nn(u, wpb[:, cols]), nt(gnb, wpo[cols, :]))
            dwpo[:, cols] += nn(gnb_t, hidden)
            dwpa[:, cols] += nn(u_t, grad_a)
            dwpb[:, cols] += nn(u_t, grad_b)
            part = nt(grad_a, wpa[:, cols]) + nt(grad_b, wpb[:, cols])
            grad_normed = part if grad_normed is None else grad_normed + part
        dzin_ref[at, :] = (grad_new + norm_grad(normed, inv, grad_normed)).astype(BF)
        for when, todo in hooks.items():
            @pl.when(b == when)
            def _():
                for red, stage in todo:
                    red.step(stage)
        return carry

    lax.fori_loop(0, num_blk, pair_backward, 0)

    for t, ref in enumerate((dwpa, dwpb, dwpo)):
        for k in range(4):
            gp[t, k * 128:(k + 1) * 128, :] = ref[:, k * LANES:(k + 1) * LANES].astype(BF)
        gp[t, 528:768, :] = jnp.zeros((240, LANES), BF)
    diag = jnp.zeros((128, LANES), F32)
    for k in range(8):
        diag = diag + jnp.where(row8 == k, m8[:, k * LANES:(k + 1) * LANES], 0.0)
    gp[0, 512:528, :] = jnp.sum(diag.reshape(HEADS, 8, LANES), axis=1).astype(BF)
    for t in range(1, 3):
        gp[t, 512:528, :] = jnp.zeros((16, LANES), BF)
    red_p.start(0)
    red_p.step(1)
    red_p.step(2)
    red_s.step(7)
    red_a.step(7)
    red_p.step(3)
    red_p.step(4)
    red_p.step(5)
    red_p.step(6)
    red_s.step(8)
    red_a.step(8)
    red_p.step(7)
    red_p.step(8)


def unpack_kernel(fs, fa, fp, pa_o, pb_o, po_o, bias_o, q_o, qb_o, kv_o, g_o, o_o, sa_o, sb_o, so_o,
                  pa, pb, po, bias, q, qb, kv, g, o, sa, sb, so, sem):
    outs = [(sa, sa_o), (sb, sb_o), (so, so_o), (q, q_o), (kv, kv_o), (g, g_o), (o, o_o), (qb, qb_o), (pa, pa_o), (pb, pb_o),
            (po, po_o), (bias, bias_o)]
    copies = [pltpu.make_async_copy(src, dst, sem.at[k]) for k, (src, dst) in enumerate(outs)]
    for t in range(3):
        for k in range(4):
            cols = slice(t * 512 + k * LANES, t * 512 + (k + 1) * LANES)
            sa[:, cols] = fs[t, k * 384:(k + 1) * 384, :].astype(F32)
    copies[0].start()
    for t in range(3):
        for k in range(4):
            cols = slice(t * 512 + k * LANES, t * 512 + (k + 1) * LANES)
            sb[:, cols] = fs[t, 1536 + k * 384:1536 + (k + 1) * 384, :].astype(F32)
    copies[1].start()
    for k in range(3):
        so[:, k * LANES:(k + 1) * LANES] = fs[k, 3072:4608, :].astype(F32)
    copies[2].start()
    for index, (ref, row) in enumerate(((q, 0), (kv, 384), (g, 1152), (o, 1536))):
        per = ref.shape[1] // 384
        for k in range(3 * per):
            lo = row + (k % per) * 384
            ref[:, k * LANES:(k + 1) * LANES] = fa[k // per, lo:lo + 384, :].astype(F32)
        copies[3 + index].start()
    for t in range(3):
        qb[:, t * LANES:(t + 1) * LANES] = fa[t, 1920:1936, :].astype(F32)[0:1]
    copies[7].start()
    for t, ref in enumerate((pa, pb)):
        for k in range(4):
            ref[:, k * LANES:(k + 1) * LANES] = fp[t, k * 128:(k + 1) * 128, :].astype(F32)
        copies[8 + t].start()
    for k in range(4):
        po[k * 128:(k + 1) * 128, :] = fp[2, k * 128:(k + 1) * 128, :].astype(F32).T
    copies[10].start()
    bias[...] = fp[0, 512:640, :].astype(F32).T[:, 0:HEADS]
    copies[11].start()
    for item in copies:
        item.wait()


def solution(mesh):
    pair_spec = P('dp', 'dap', None, None)
    single_spec = P('dp', 'dap', None)
    hbm = pl.BlockSpec(memory_space=pl.ANY)
    vmem = pl.BlockSpec(memory_space=pltpu.VMEM)

    def body(pair_z, single_s, token_mask, dz_out, ds_out, w_pa, w_pb, w_po, w_bias, w_q, q_bias, w_kv, w_g, w_o, w_sa, w_sb, w_so):
        num_cplx, half, num_tok, dim = pair_z.shape
        toks = num_cplx * half * num_tok
        rows = num_cplx * half
        width = w_q.shape[1]
        big = (pair_z.reshape(toks, dim), dz_out.reshape(toks, dim), w_pa, w_pb, w_po, w_q, w_kv, w_g, w_o, w_sa, w_sb, w_so)
        small = (single_s.reshape(rows, width), ds_out.reshape(rows, width), token_mask, q_bias.reshape(1, width), w_bias)
        scratch = [pltpu.VMEM(a.shape, a.dtype) for a in big]
        scratch += [
            pltpu.VMEM((toks, dim), BF), pltpu.VMEM((128, 1024), BF),
            pltpu.VMEM((num_cplx, HEADS, half, num_tok), F32), pltpu.VMEM((num_cplx, HEADS * half, num_tok), F32),
            pltpu.VMEM((rows, width), BF), pltpu.VMEM((rows, width), BF), pltpu.VMEM((rows, width), F32),
            pltpu.VMEM((rows, width), F32), pltpu.VMEM((rows, width), BF), pltpu.VMEM((rows, width), BF),
            pltpu.VMEM((rows, width), F32),
            pltpu.VMEM((2, rows, 2 * width), BF), pltpu.VMEM((2, rows, 2 * width), BF), pltpu.VMEM((rows, 2 * width), BF),
            pltpu.VMEM((128, 512), F32), pltpu.VMEM((128, 512), F32), pltpu.VMEM((128, 512), F32), pltpu.VMEM((128, 1024), F32),
        ]
        for total in (ROWS_S, ROWS_A, ROWS_P):
            scratch += [pltpu.VMEM((3, total >> k, LANES), BF) for k in range(5)]
        scratch += [pltpu.SemaphoreType.DMA((12,)), pltpu.SemaphoreType.DMA((4,)),
                    pltpu.SemaphoreType.DMA((3, 8, 3)), pltpu.SemaphoreType.DMA((3, 8, 3))]
        dz_in, ds_in, fs, fa, fp = pl.pallas_call(
            body_kernel,
            out_shape=[jax.ShapeDtypeStruct((toks, dim), BF), jax.ShapeDtypeStruct((rows, width), BF)] + [
                jax.ShapeDtypeStruct((3, total, LANES), BF) for total in (ROWS_S, ROWS_A, ROWS_P)],
            in_specs=[hbm] * 12 + [vmem] * 5,
            out_specs=[vmem] * 5,
            scratch_shapes=scratch,
            compiler_params=pltpu.CompilerParams(collective_id=0, has_side_effects=True, vmem_limit_bytes=60 * 2 ** 20),
            name="block",
        )(*big, *small)
        shapes = [w_pa.shape, w_pb.shape, w_po.shape, w_bias.shape, w_q.shape, (1, width), w_kv.shape, w_g.shape, w_o.shape,
                  w_sa.shape, w_sb.shape, w_so.shape]
        grads = pl.pallas_call(
            unpack_kernel,
            out_shape=[jax.ShapeDtypeStruct(shape, F32) for shape in shapes],
            in_specs=[vmem] * 3,
            out_specs=[hbm] * 12,
            scratch_shapes=[pltpu.VMEM(shape, F32) for shape in shapes] + [pltpu.SemaphoreType.DMA((12,))],
            compiler_params=pltpu.CompilerParams(vmem_limit_bytes=40 * 2 ** 20),
            name="unpack",
        )(fs, fa, fp)
        grads = list(grads)
        grads[5] = grads[5].reshape(width)
        return (dz_in.reshape(pair_z.shape), ds_in.reshape(single_s.shape)) + tuple(grads)

    in_specs = (pair_spec, single_spec, P('dp', None), pair_spec, single_spec) + (P(),) * 12
    out_specs = (pair_spec, single_spec) + (P(),) * 12
    return jax.shard_map(body, mesh=mesh, in_specs=in_specs, out_specs=out_specs, check_vma=False)
```

time: 378 us -> 119 us (0.31)
  matrix products: 130 us -> 0 us
  Pallas kernels: 0 us -> 108 us
  waiting for transfers between devices: 103 us -> 0 us
  other arithmetic: 52.1 us -> 0.6 us
  blocking collectives: 42 us -> 0 us
  local copies, waits for them, and re-layouts: 32.1 us -> 9.56 us
  between operations: 14.7 us -> 0.68 us
    dot_general x104 -> x0, matrix products: 130 us -> none  [contract(): jnp.einsum(equation, left_op, right_op, preferred_element_type=jnp.float32)]
    pallas_call x0 -> x2, Pallas kernels: none -> 108 us  [the longest x1 103 us: body(): pl.pallas_call(body_kernel, out_shape=[jax.ShapeDtypeStruct((toks, dim),...]
    psum x1 -> x0, waiting for transfers between devices: 103 us -> none  [body(): lax.psum(pair_grads + (d_w_q, d_q_bias, d_w_kv, d_w_g, d_w_o, d_w_sa, d_w...]
    psum x1 -> x0, blocking collectives: 34.2 us -> none  [body(): lax.psum(pair_grads + (d_w_q, d_q_bias, d_w_kv, d_w_g, d_w_o, d_w_sa, d_w...]
    reduce_sum x46 -> x0, other arithmetic: 28 us -> none  [the longest x26 16.3 us: layer_norm(): jnp.mean(centred * centred, axis=-1, keepdims=True) + EPSILON]
    add x7 -> x0, other arithmetic: 9.98 us -> none  [the longest x6 9.86 us: pair_backward(): dz_rows.astype(jnp.float32) + norm_grad(bias_norm, bias_inv, grad_norm)]
    unnamed x122 -> x14, local copies, waits for them, and re-layouts: 17.6 us -> 8.32 us
    dynamic_update_slice x6 -> x0, other arithmetic: 7.94 us -> none  [body(): z_new, bias_rows = lax.map(forward_rows, z_blocks)]
  transfers between devices with their start and end apart: 2 -> 0, of which waited for: 1 -> 0; matrix products, arithmetic and copies ran while one was open for 30% -> 0% of each run, Pallas kernels for 0% -> 0%
where the time goes in v1:
time: 119 us
  Pallas kernels  108 us (91%)
  local copies, waits for them, and re-layouts  9.56 us (8%)
    pallas_call x1, Pallas kernels, body(): pl.pallas_call(body_kernel, out_shape=[jax.ShapeDtypeStruct((toks, dim),...  103 us
    unnamed x14, local copies, waits for them, and re-layouts  8.32 us
    pallas_call x1, Pallas kernels, body(): pl.pallas_call(unpack_kernel, out_shape=[jax.ShapeDtypeStruct(shape, F32)...  4.41 us

profile of v1, /device:TPU:0, one launch (start us, length us, event | category | flops | bytes accessed | tf_op | source)
XLA Modules:
  0.0 118.5 jit_solution(8425597682676944427)
XLA Ops:
  0.6 1.2 %reshape.56.qb_ref = bf16[1,384]{1,0:T(2,128)(2,1)} reshape(bf16[384]{0:T(512)(128)(2,1)} %param.27) | data formatting | bytes 1536 | tf_op jit(solution)/shard_map/reshape | solution.py:443
  1.9 1.4 %copy.31.wbias_ref = bf16[128,16]{1,0:T(8,128)(2,1)} copy(bf16[128,16]{0,1:T(8,128)(2,1)} %param.25) | data formatting | bytes 8192 | tf_op args[8]
  3.3 103.3 %block.1 = (bf16[6144,128]{1,0:T(8,128)(2,1)}, bf16[96,384]{1,0:T(8,128)(2,1)}, bf16[3,4608,128]{2,1,0:T(8,128)(2,1)}, bf16[3,2048,128]{2,1,0:T(8,128)(2,1)}, bf16[3,768,128]{2,1,0:T(8,128)(2,1)}) custom-call(bf16[6144,128]{1,0:T(8,128)(2,1)} %bitcast.7, bf16[6144,128]{1,0:T(8,128)(2,1)} %bitcast.8, bf16[128,512]{1,0:T(8,128)(2,1)} %wpa_hbm.1, ...), custom_call_target="tpu_custom_call" | custom-call | tf_op jit(solution)/shard_map/block/pallas_call | solution.py:458
  106.6 0.0 copy-start
  106.6 2.0 %copy-done = bf16[3,4608,128]{2,1,0:T(8,128)(2,1)S(1)} copy-done((bf16[3,4608,128]{2,1,0:T(8,128)(2,1)S(1)}, bf16[3,4608,128]{2,1,0:T(8,128)(2,1)}, u32[]{:S(2)}) %copy-start) | copy-done | bytes 3538968
  108.6 0.0 copy-start.1
  108.6 1.4 %copy-done.1 = bf16[3,2048,128]{2,1,0:T(8,128)(2,1)S(1)} copy-done((bf16[3,2048,128]{2,1,0:T(8,128)(2,1)S(1)}, bf16[3,2048,128]{2,1,0:T(8,128)(2,1)}, u32[]{:S(2)}) %copy-start.1) | copy-done | bytes 1572888
  110.0 0.0 copy-start.2
  110.0 1.1 copy-done.2
  111.1 0.0 copy-start.3
  111.1 4.4 %unpack.1 = (f32[128,512]{1,0:T(8,128)}, f32[128,512]{1,0:T(8,128)}, f32[512,128]{1,0:T(8,128)}, f32[128,16]{1,0:T(8,128)S(1)}, f32[384,384]{1,0:T(8,128)}, /*in...) custom-call(bf16[3,4608,128]{2,1,0:T(8,128)(2,1)S(1)} %copy-done, ...), custom_call_target="tpu_custom_call" | custom-call | tf_op jit(solution)/shard_map/unpack/pallas_call | solution.py:470
  115.5 0.6 reduce
  116.1 0.7 copy.32
  116.7 0.0 copy-done.3
  116.7 0.0 copy-start.4
  116.7 1.1 copy.35
  117.9 0.0 copy-done.4
  117.9 0.6 copy.36
Async XLA Ops:
  106.6 2.0 %copy-start = (bf16[3,4608,128]{2,1,0:T(8,128)(2,1)S(1)}, bf16[3,4608,128]{2,1,0:T(8,128)(2,1)}, u32[]{:S(2)}) copy-start(bf16[3,4608,128]{2,1,0:T(8,128)(2,1)} %get-tuple-element.33.fs) | copy-start | bytes 10616836
  108.6 1.4 %copy-start.1 = (bf16[3,2048,128]{2,1,0:T(8,128)(2,1)S(1)}, bf16[3,2048,128]{2,1,0:T(8,128)(2,1)}, u32[]{:S(2)}) copy-start(bf16[3,2048,128]{2,1,0:T(8,128)(2,1)} %get-tuple-element.34.fa) | copy-start | bytes 4718596
  110.0 1.1 copy-start.2
  111.1 5.7 %copy-start.3 = (bf16[6144,128]{1,0:T(8,128)(2,1)S(1)}, bf16[6144,128]{1,0:T(8,128)(2,1)}, u32[]{:S(2)}) copy-start(bf16[6144,128]{1,0:T(8,128)(2,1)} %get-tuple-element.31) | copy-start | bytes 4718596
  116.7 1.1 copy-start.4

commit v2 on v1

--- a/solution.py
+++ b/solution.py
@@ -11,7 +11,7 @@
 MASK_BIG = 1e9
 BF = jnp.bfloat16
 F32 = jnp.float32
-ROWS_S, ROWS_A, ROWS_P = 4608, 2048, 768
+ROWS_A, ROWS_P = 2048, 544
 LANES = 128
 
 
@@ -51,21 +51,33 @@
     return hidden.astype(BF), grad_a.astype(BF), (dh * silu).astype(BF)
 
 
+AXES = ("x", "y", "z")
+ORDER = (("x", "y", "z"), ("y", "z", "x"), ("z", "x", "y"))
+ORDER_YZ = (("y", "z"), ("z", "y"), ("y", "z"))
+
+
+def remote(place, src, dst, send_sem, recv_sem, axis):
+    return pltpu.make_async_remote_copy(
+        src_ref=src, dst_ref=dst, send_sem=send_sem, recv_sem=recv_sem,
+        device_id=place["peers"][axis], device_id_type=pl.DeviceIdType.MESH)
+
+
 class Reducer:
+    last = 8
+
     def __init__(self, place, rows, grads, recvs, final, send_sem, recv_sem):
         self.place, self.rows, self.grads, self.recvs, self.final = place, rows, grads, recvs, final
         self.send_sem, self.recv_sem = send_sem, recv_sem
         coords = place["coords"]
-        self.order = [("x", "y", "z"), ("y", "z", "x"), ("z", "x", "y")]
         self.base = []
         for third in range(3):
             base = [coords["core"] * (rows // 2)]
-            for depth, axis in enumerate(self.order[third]):
+            for depth, axis in enumerate(ORDER[third]):
                 base.append(base[-1] + coords[axis] * (rows >> (depth + 2)))
             self.base.append(base)
 
     def copy(self, stage, third):
-        rows, base, order = self.rows, self.base[third], self.order[third]
+        rows, base, order = self.rows, self.base[third], ORDER[third]
         coords = self.place["coords"]
         step = rows // 16
         if stage < 4:
@@ -81,46 +93,120 @@
             start = pl.multiple_of(base[7 - stage], step)
             src = self.final.at[third, pl.ds(start, size)]
             dst = src
-        return pltpu.make_async_remote_copy(
-            src_ref=src, dst_ref=dst,
-            send_sem=self.send_sem.at[stage, third], recv_sem=self.recv_sem.at[stage, third],
-            device_id=self.place["peers"][axis], device_id_type=pl.DeviceIdType.MESH)
-
-    def start(self, stage):
+        return remote(self.place, src, dst, self.send_sem.at[stage, third], self.recv_sem.at[stage, third], axis)
+
+    def add(self, third, low, size, chunk, recv, dest):
+        def run(k, carry):
+            at = pl.ds(pl.multiple_of(low + k * chunk, chunk), chunk)
+            off = pl.ds(pl.multiple_of(k * chunk, chunk), chunk)
+            dest[third, at, :] = (self.grads[third, at, :].astype(F32) + recv[third, off, :].astype(F32)).astype(BF)
+            return carry
+
+        lax.fori_loop(0, size // chunk, run, 0)
+
+    def start(self):
         for third in range(3):
-            self.copy(stage, third).start()
+            self.copy(0, third).start()
 
     def step(self, stage):
         for third in range(3):
             done = stage - 1
             self.copy(done, third).wait()
             if done < 4:
-                size = self.rows >> (done + 1)
-                chunk = self.rows // 16
-                low = self.base[third][done]
-                dest = self.final if done == 3 else self.grads
-                recv = self.recvs[done]
-
-                def add(k, carry):
-                    at = pl.ds(pl.multiple_of(low + k * chunk, chunk), chunk)
-                    off = pl.ds(pl.multiple_of(k * chunk, chunk), chunk)
-                    dest[third, at, :] = (self.grads[third, at, :].astype(F32) + recv[third, off, :].astype(F32)).astype(BF)
-                    return carry
-
-                lax.fori_loop(0, size // chunk, add, 0)
-            if stage < 8:
+                self.add(third, self.base[third][done], self.rows >> (done + 1), self.rows // 16, self.recvs[done],
+                         self.final if done == 3 else self.grads)
+            if stage < self.last:
                 self.copy(stage, third).start()
+
+
+class Doubler(Reducer):
+    last = 5
+
+    def copy(self, stage, third):
+        half = self.rows // 2
+        core = self.place["coords"]["core"]
+        mine = pl.ds(pl.multiple_of(core * half, 16), half)
+        if stage == 0:
+            src = self.grads.at[third, pl.ds(pl.multiple_of((1 - core) * half, 16), half)]
+            dst, axis = self.recvs[0].at[third], "core"
+        elif stage < 4:
+            src, dst, axis = self.grads.at[third, mine], self.recvs[stage].at[third], ORDER[third][stage - 1]
+        else:
+            src, dst, axis = self.final.at[third, mine], self.final.at[third, mine], "core"
+        return remote(self.place, src, dst, self.send_sem.at[stage, third], self.recv_sem.at[stage, third], axis)
+
+    def step(self, stage):
+        half = self.rows // 2
+        for third in range(3):
+            done = stage - 1
+            self.copy(done, third).wait()
+            if done < 4:
+                self.add(third, self.base[third][0], half, half, self.recvs[done], self.final if done == 3 else self.grads)
+            if stage < self.last:
+                self.copy(stage, third).start()
+
+
+class Gatherer:
+    def __init__(self, place, buf, send_sem, recv_sem):
+        self.place, self.buf, self.send_sem, self.recv_sem = place, buf, send_sem, recv_sem
+
+    def copy(self, stage, third):
+        coords, order = self.place["coords"], ORDER[third]
+        got = order[:stage - 1]
+        index = [third, coords["core"]] + [slice(None) if axis in got else coords[axis] for axis in AXES]
+        ref = self.buf.at[tuple(index)]
+        axis = order[stage - 1] if stage < 4 else "core"
+        return remote(self.place, ref, ref, self.send_sem.at[stage, third], self.recv_sem.at[stage, third], axis)
+
+    def step(self, stage):
+        for third in range(3):
+            if stage > 1:
+                self.copy(stage - 1, third).wait()
+            if stage < 5:
+                self.copy(stage, third).start()
+
+
+class Tiles:
+    def __init__(self, place, buf0, buf1, send_sem, recv_sem):
+        self.place, self.bufs, self.send_sem, self.recv_sem = place, (buf0, buf1), send_sem, recv_sem
+
+    def copy(self, core, stage, third):
+        coords = self.place["coords"]
+        order = ORDER[third] if core == 0 else ORDER_YZ[third]
+        axes = AXES if core == 0 else AXES[1:]
+        if stage > len(order):
+            ref, axis, slot = self.bufs[core].at[third], "core", 4 + core
+        else:
+            got = order[:stage - 1]
+            ref = self.bufs[core].at[tuple([third] + [slice(None) if axis in got else coords[axis] for axis in axes])]
+            axis, slot = order[stage - 1], stage
+        return remote(self.place, ref, ref, self.send_sem.at[slot, third], self.recv_sem.at[slot, third], axis)
+
+    def step(self, stage):
+        for core in range(2):
+            last = 4 - core
+
+            @pl.when(self.place["coords"]["core"] == core)
+            def _():
+                for third in range(3):
+                    if 1 < stage <= last:
+                        self.copy(core, stage - 1, third).wait()
+                    if stage <= last:
+                        self.copy(core, stage, third).start()
+                    if stage == 5:
+                        self.copy(core, last, third).wait_send()
+                        self.copy(1 - core, 3 + core, third).wait_recv()
 
 
 def body_kernel(
         z_hbm, dz_hbm, wpa_hbm, wpb_hbm, wpo_hbm, wq_hbm, wkv_hbm, wg_hbm, wo_hbm, wsa_hbm, wsb_hbm, wso_hbm,
         s_ref, ds_ref, mask_ref, qb_ref, wbias_ref,
-        dzin_ref, dsin_ref, fs_ref, fa_ref, fp_ref,
+        dzin_hbm, dsin_hbm, fs0_hbm, fs1_hbm, fa_hbm, fp_hbm,
         z_v, dz_v, wpa, wpb, wpo, wq, wkv, wg, wo, wsa, wsb, wso,
         z1_v, w8, bias_v, prob_v, act_v, q_v, gate_v, att_v, gated_v, gatt_v, gmid_v, kv_v, gkv_v, gkvr_v,
-        dwpa, dwpb, dwpo, m8,
-        gs, gs0, gs1, gs2, gs3, ga_, ga0, ga1, ga2, ga3, gp, gp0, gp1, gp2, gp3,
-        in_sem, kv_sem, send_sem, recv_sem):
+        dwpa, dwpb, dwpo, m8, dzin_ref, dsin_ref, c_all, ds_all, d_ab, d_so, fs0, fs1, fa_ref, fp_ref,
+        ga_, ga0, ga1, ga2, ga3, gp, gp0, gp1, gp2, gp3,
+        in_sem, out_sem, dz_sem, kv_sem, send_sem, recv_sem):
     dap = lax.axis_index("dap")
     dp = lax.axis_index("dp")
     core = lax.rem(dp, 2)
@@ -148,9 +234,18 @@
         pl.semaphore_signal(barrier, inc=1, device_id=peer, device_id_type=pl.DeviceIdType.MESH)
     pl.semaphore_wait(barrier, 4)
 
-    red_s = Reducer(place, ROWS_S, gs, (gs0, gs1, gs2, gs3), fs_ref, send_sem.at[0], recv_sem.at[0])
-    red_a = Reducer(place, ROWS_A, ga_, (ga0, ga1, ga2, ga3), fa_ref, send_sem.at[1], recv_sem.at[1])
-    red_p = Reducer(place, ROWS_P, gp, (gp0, gp1, gp2, gp3), fp_ref, send_sem.at[2], recv_sem.at[2])
+    red_a = Reducer(place, ROWS_A, ga_, (ga0, ga1, ga2, ga3), fa_ref, send_sem.at[0], recv_sem.at[0])
+    red_p = Doubler(place, ROWS_P, gp, (gp0, gp1, gp2, gp3), fp_ref, send_sem.at[1], recv_sem.at[1])
+    gat_ds = Gatherer(place, ds_all, send_sem.at[2], recv_sem.at[2])
+    gat_c = Gatherer(place, c_all, send_sem.at[3], recv_sem.at[3])
+    tiles = Tiles(place, fs0, fs1, send_sem.at[4], recv_sem.at[4])
+
+    def own_block(buf, value):
+        for t in range(3):
+            buf[t, core, cx, cy, dap] = value[:, t * LANES:(t + 1) * LANES]
+
+    own_block(ds_all, ds_ref[...])
+    gat_ds.step(1)
 
     s_f = s_ref[...].astype(F32)
     s_norm, s_inv = layer_norm(s_f)
@@ -172,13 +267,13 @@
     kv_copy().start()
     copies[1].wait()
     copies[2].wait()
-    q_v[...] = (nn(act, wq[...]) + qb_ref[...].astype(F32)).astype(BF)
+    q_v[...] = (nn(act, wq[...]) + qb_ref[...].astype(F32).reshape(1, width)).astype(BF)
     gate_v[...] = sigmoid(nn(act, wg[...]))
 
     row_head = lax.broadcasted_iota(jnp.int32, (128, HEADS), 0)
     col_head = lax.broadcasted_iota(jnp.int32, (128, HEADS), 1)
     pick = jnp.where((row_head >= col_head * 8) & (row_head < col_head * 8 + 8), 1.0, 0.0).astype(BF)
-    spread = nt(pick, wbias_ref[...])
+    spread = nn(pick, wbias_ref[...])
     row8 = lax.rem(lax.broadcasted_iota(jnp.int32, (128, LANES), 0), 8)
     for k in range(8):
         w8[:, k * LANES:(k + 1) * LANES] = jnp.where(row8 == k, spread, 0.0).astype(BF)
@@ -210,6 +305,10 @@
         bias8 = nt(w8[...], side_by_side(bias_norm.astype(BF)))
         c, i0 = b // per_cplx, pl.multiple_of(lax.rem(b, per_cplx) * 8, 8)
         bias_v[c, :, pl.ds(i0, 8), :] = bias8.reshape(HEADS, 8, num_tok)
+        for when, stage in ((2, 2), (5, 3), (9, 4)):
+            @pl.when(b == when)
+            def _():
+                gat_ds.step(stage)
         return carry
 
     lax.fori_loop(0, num_blk, pair_forward, 0)
@@ -245,7 +344,9 @@
     s_mid = (s_ref[...].astype(F32) + nn(gated, wo[...])).astype(BF)
     mid_norm, mid_inv = layer_norm(s_mid.astype(F32))
     mid_act = mid_norm.astype(BF)
-    mid_t = mid_act.T
+    own_block(c_all, mid_act)
+    gat_c.step(1)
+    gat_ds.step(5)
 
     for k in range(8, 11):
         copies[k].wait()
@@ -256,18 +357,9 @@
         ta = nn(mid_act, wsa[:, cols])
         tb = nn(mid_act, wsb[:, cols])
         dh = nt(ds_b, wso[cols, :])
-        hidden, grad_a, grad_b = swiglu_grad(ta, tb, dh)
+        _, grad_a, grad_b = swiglu_grad(ta, tb, dh)
         part = nt(grad_a, wsa[:, cols]) + nt(grad_b, wsb[:, cols])
         grad_mid_norm = part if grad_mid_norm is None else grad_mid_norm + part
-        d_sa = nn(mid_t, grad_a).astype(BF)
-        d_sb = nn(mid_t, grad_b).astype(BF)
-        for k in range(4):
-            gs[t, k * 384:(k + 1) * 384, :] = d_sa[:, k * LANES:(k + 1) * LANES]
-            gs[t, 1536 + k * 384:1536 + (k + 1) * 384, :] = d_sb[:, k * LANES:(k + 1) * LANES]
-        d_so = tn(hidden, ds_b).astype(BF)
-        for k in range(3):
-            gs[k, 3072 + t * 512:3072 + (t + 1) * 512, :] = d_so[:, k * LANES:(k + 1) * LANES]
-    red_s.start(0)
     grad_mid = ds_b.astype(F32) + norm_grad(mid_norm, mid_inv, grad_mid_norm)
     gmid_v[...] = grad_mid
     grad_mid_bf = grad_mid.astype(BF)
@@ -283,6 +375,7 @@
             lo = name_row + (k % per) * 384
             ga_[k // per, lo:lo + 384, :] = val[:, k * LANES:(k + 1) * LANES]
 
+    gat_c.step(2)
     act_t = act_v[...].T
     put_attn(1152, nn(act_t, grad_gate_pre))
     put_attn(1536, tn(gated_v[...], grad_mid_bf))
@@ -303,8 +396,6 @@
         for d in range(2):
             gkv_v[d, rows, 0:width] = grad_keys[d * half:(d + 1) * half].astype(BF)
             gkv_v[d, rows, width:2 * width] = grad_vals[d * half:(d + 1) * half].astype(BF)
-        if c == 1:
-            red_s.step(1)
     gkv_copy().start()
     grad_q = jnp.concatenate(grad_q_parts, axis=0)
     grad_q_bf = grad_q.astype(BF)
@@ -318,17 +409,71 @@
     gkv_copy().wait()
     grad_kv = (gkv_v[dap].astype(F32) + gkvr_v[...].astype(F32)).astype(BF)
     put_attn(384, nn(act_t, grad_kv))
-    red_a.start(0)
+    red_a.start()
+    gat_c.step(3)
     grad_act = grad_act + nt(grad_kv, wkv[...])
     s_norm2, s_inv2 = layer_norm(s_ref[...].astype(F32))
     dsin_ref[...] = (gmid_v[...] + norm_grad(s_norm2, s_inv2, grad_act)).astype(BF)
+    outs = [(dsin_ref, dsin_hbm), (fs0, fs0_hbm), (fs1, fs1_hbm), (fa_ref, fa_hbm), (fp_ref, fp_hbm)]
+    out_copies = [pltpu.make_async_copy(src, dst, out_sem.at[k]) for k, (src, dst) in enumerate(outs)]
+    out_copies[0].start()
+
+    def tile_grads():
+        tile = jnp.where(core == 0, 3 * (2 * cy + dap) + 2 * cx, 3 * (2 * cy + dap) + 1)
+        at = pl.ds(pl.multiple_of(tile * LANES, LANES), LANES)
+        w_ab = jnp.concatenate([wsa[:, at], wsb[:, at]], axis=1)
+        w_o_tile = wso[at, :]
+        d_ab[...] = jnp.zeros(d_ab.shape, F32)
+        d_so[...] = jnp.zeros(d_so.shape, F32)
+
+        def quarter(k, carry):
+            def rows_of(buf):
+                return jnp.concatenate([buf[t, k // 2, lax.rem(k, 2)].reshape(4 * 96, LANES) for t in range(3)], axis=1)
+
+            acts, cots = rows_of(c_all), rows_of(ds_all)
+            both = nn(acts, w_ab)
+            hidden, grad_a, grad_b = swiglu_grad(both[:, :LANES], both[:, LANES:], nt(cots, w_o_tile))
+            d_ab[...] += tn(acts, jnp.concatenate([grad_a, grad_b], axis=1))
+            d_so[...] += tn(hidden, cots)
+            return carry
+
+        lax.fori_loop(0, 4, quarter, 0)
+        for k in range(2):
+            @pl.when(core == k)
+            def _():
+                slot = (cx, cy, dap) if k == 0 else (cy, dap)
+                buf = fs0 if k == 0 else fs1
+                buf[(0,) + slot] = d_ab[:, :LANES].astype(BF)
+                buf[(1,) + slot] = d_ab[:, LANES:].astype(BF)
+                so_b = d_so[...].astype(BF)
+                buf[(2,) + slot] = jnp.concatenate([so_b[:, t * LANES:(t + 1) * LANES] for t in range(3)], axis=0)
 
     copies[11].wait()
     for ref in (dwpa, dwpb, dwpo, m8):
         ref[...] = jnp.zeros(ref.shape, F32)
 
-    hooks = {0: [(red_a, 1)], 2: [(red_s, 2)], 3: [(red_a, 2)], 5: [(red_s, 3), (red_a, 3)], 7: [(red_s, 4), (red_a, 4)],
-             9: [(red_s, 5), (red_a, 5)], 11: [(red_s, 6), (red_a, 6)]}
+    def hook(*calls):
+        def run():
+            for call in calls:
+                call()
+        return run
+
+    def dz_copy(k):
+        at = pl.ds(pl.multiple_of(k * blk, blk), blk)
+        return pltpu.make_async_copy(dzin_ref.at[at, :], dzin_hbm.at[at, :], dz_sem.at[k])
+
+    hooks = {
+        0: hook(lambda: red_a.step(1)),
+        2: hook(lambda: gat_c.step(4), lambda: red_a.step(2)),
+        3: hook(lambda: gat_c.step(5), tile_grads, lambda: tiles.step(1)),
+        4: hook(lambda: red_a.step(3)),
+        5: hook(lambda: tiles.step(2)),
+        6: hook(lambda: red_a.step(4)),
+        7: hook(lambda: tiles.step(3)),
+        8: hook(lambda: red_a.step(5)),
+        10: hook(lambda: red_a.step(6)),
+        11: hook(lambda: tiles.step(4)),
+    }
 
     def pair_backward(b, carry):
         at = pl.ds(pl.multiple_of(b * blk, blk), blk)
@@ -354,11 +499,9 @@
             part = nt(grad_a, wpa[:, cols]) + nt(grad_b, wpb[:, cols])
             grad_normed = part if grad_normed is None else grad_normed + part
         dzin_ref[at, :] = (grad_new + norm_grad(normed, inv, grad_normed)).astype(BF)
+        dz_copy(b).start()
         for when, todo in hooks.items():
-            @pl.when(b == when)
-            def _():
-                for red, stage in todo:
-                    red.step(stage)
+            pl.when(b == when)(todo)
         return carry
 
     lax.fori_loop(0, num_blk, pair_backward, 0)
@@ -366,46 +509,63 @@
     for t, ref in enumerate((dwpa, dwpb, dwpo)):
         for k in range(4):
             gp[t, k * 128:(k + 1) * 128, :] = ref[:, k * LANES:(k + 1) * LANES].astype(BF)
-        gp[t, 528:768, :] = jnp.zeros((240, LANES), BF)
+        gp[t, 528:544, :] = jnp.zeros((16, LANES), BF)
     diag = jnp.zeros((128, LANES), F32)
     for k in range(8):
         diag = diag + jnp.where(row8 == k, m8[:, k * LANES:(k + 1) * LANES], 0.0)
     gp[0, 512:528, :] = jnp.sum(diag.reshape(HEADS, 8, LANES), axis=1).astype(BF)
     for t in range(1, 3):
         gp[t, 512:528, :] = jnp.zeros((16, LANES), BF)
-    red_p.start(0)
+    red_p.start()
     red_p.step(1)
+    red_a.step(7)
     red_p.step(2)
-    red_s.step(7)
-    red_a.step(7)
+    tiles.step(5)
+    out_copies[1].start()
+    out_copies[2].start()
+    red_a.step(8)
+    out_copies[3].start()
     red_p.step(3)
     red_p.step(4)
     red_p.step(5)
-    red_p.step(6)
-    red_s.step(8)
-    red_a.step(8)
-    red_p.step(7)
-    red_p.step(8)
-
-
-def unpack_kernel(fs, fa, fp, pa_o, pb_o, po_o, bias_o, q_o, qb_o, kv_o, g_o, o_o, sa_o, sb_o, so_o,
-                  pa, pb, po, bias, q, qb, kv, g, o, sa, sb, so, sem):
+    out_copies[4].start()
+
+    def drain(k, carry):
+        dz_copy(k).wait()
+        return carry
+
+    lax.fori_loop(0, num_blk, drain, 0)
+    for item in out_copies:
+        item.wait()
+
+
+def unpack_kernel(dz_i, ds_i, fs0_i, fs1_i, fa_i, fp_i,
+                  dz_o, ds_o, pa_o, pb_o, po_o, bias_o, q_o, qb_o, kv_o, g_o, o_o, sa_o, sb_o, so_o,
+                  dz, ds, fs0, fs1, fa, fp, pa, pb, po, bias, q, qb, kv, g, o, sa, sb, so, in_sem, sem):
+    ins = [(fs0_i, fs0), (fs1_i, fs1), (fa_i, fa), (fp_i, fp), (dz_i, dz), (ds_i, ds)]
+    reads = [pltpu.make_async_copy(src, dst, in_sem.at[k]) for k, (src, dst) in enumerate(ins)]
+    for item in reads:
+        item.start()
     outs = [(sa, sa_o), (sb, sb_o), (so, so_o), (q, q_o), (kv, kv_o), (g, g_o), (o, o_o), (qb, qb_o), (pa, pa_o), (pb, pb_o),
-            (po, po_o), (bias, bias_o)]
+            (po, po_o), (bias, bias_o), (dz, dz_o), (ds, ds_o)]
     copies = [pltpu.make_async_copy(src, dst, sem.at[k]) for k, (src, dst) in enumerate(outs)]
-    for t in range(3):
-        for k in range(4):
-            cols = slice(t * 512 + k * LANES, t * 512 + (k + 1) * LANES)
-            sa[:, cols] = fs[t, k * 384:(k + 1) * 384, :].astype(F32)
-    copies[0].start()
-    for t in range(3):
-        for k in range(4):
-            cols = slice(t * 512 + k * LANES, t * 512 + (k + 1) * LANES)
-            sb[:, cols] = fs[t, 1536 + k * 384:1536 + (k + 1) * 384, :].astype(F32)
-    copies[1].start()
-    for k in range(3):
-        so[:, k * LANES:(k + 1) * LANES] = fs[k, 3072:4608, :].astype(F32)
-    copies[2].start()
+
+    reads[0].wait()
+    reads[1].wait()
+    for kind in range(3):
+        for pair in range(4):
+            cy, cz = pair // 2, pair % 2
+            for j in range(3):
+                lo = (3 * pair + j) * LANES
+                tile = fs1[kind, cy, cz] if j == 1 else fs0[kind, j // 2, cy, cz]
+                wide = tile.astype(F32)
+                if kind < 2:
+                    (sa, sb)[kind][:, lo:lo + LANES] = wide
+                else:
+                    for k in range(3):
+                        so[lo:lo + LANES, k * LANES:(k + 1) * LANES] = wide[k * LANES:(k + 1) * LANES]
+        copies[kind].start()
+    reads[2].wait()
     for index, (ref, row) in enumerate(((q, 0), (kv, 384), (g, 1152), (o, 1536))):
         per = ref.shape[1] // 384
         for k in range(3 * per):
@@ -413,8 +573,9 @@
             ref[:, k * LANES:(k + 1) * LANES] = fa[k // per, lo:lo + 384, :].astype(F32)
         copies[3 + index].start()
     for t in range(3):
-        qb[:, t * LANES:(t + 1) * LANES] = fa[t, 1920:1936, :].astype(F32)[0:1]
+        qb[t * LANES:(t + 1) * LANES] = fa[t, 1920:1936, :].astype(F32)[0]
     copies[7].start()
+    reads[3].wait()
     for t, ref in enumerate((pa, pb)):
         for k in range(4):
             ref[:, k * LANES:(k + 1) * LANES] = fp[t, k * 128:(k + 1) * 128, :].astype(F32)
@@ -422,8 +583,11 @@
     for k in range(4):
         po[k * 128:(k + 1) * 128, :] = fp[2, k * 128:(k + 1) * 128, :].astype(F32).T
     copies[10].start()
-    bias[...] = fp[0, 512:640, :].astype(F32).T[:, 0:HEADS]
+    bias[...] = fp[0, 512:528, :].astype(F32)
     copies[11].start()
+    for k in range(2):
+        reads[4 + k].wait()
+        copies[12 + k].start()
     for item in copies:
         item.wait()
 
@@ -440,8 +604,9 @@
         rows = num_cplx * half
         width = w_q.shape[1]
         big = (pair_z.reshape(toks, dim), dz_out.reshape(toks, dim), w_pa, w_pb, w_po, w_q, w_kv, w_g, w_o, w_sa, w_sb, w_so)
-        small = (single_s.reshape(rows, width), ds_out.reshape(rows, width), token_mask, q_bias.reshape(1, width), w_bias)
+        small = (single_s.reshape(rows, width), ds_out.reshape(rows, width), token_mask, q_bias, w_bias.T)
         scratch = [pltpu.VMEM(a.shape, a.dtype) for a in big]
+        finals = [(toks, dim), (rows, width), (3, 2, 2, 2, width, LANES), (3, 2, 2, width, LANES), (3, ROWS_A, LANES), (3, ROWS_P, LANES)]
         scratch += [
             pltpu.VMEM((toks, dim), BF), pltpu.VMEM((128, 1024), BF),
             pltpu.VMEM((num_cplx, HEADS, half, num_tok), F32), pltpu.VMEM((num_cplx, HEADS * half, num_tok), F32),
@@ -450,35 +615,39 @@
             pltpu.VMEM((rows, width), F32),
             pltpu.VMEM((2, rows, 2 * width), BF), pltpu.VMEM((2, rows, 2 * width), BF), pltpu.VMEM((rows, 2 * width), BF),
             pltpu.VMEM((128, 512), F32), pltpu.VMEM((128, 512), F32), pltpu.VMEM((128, 512), F32), pltpu.VMEM((128, 1024), F32),
+            pltpu.VMEM(finals[0], BF), pltpu.VMEM(finals[1], BF),
+            pltpu.VMEM((3, 2, 2, 2, 2, rows, LANES), BF), pltpu.VMEM((3, 2, 2, 2, 2, rows, LANES), BF),
+            pltpu.VMEM((width, 2 * LANES), F32), pltpu.VMEM((LANES, width), F32),
         ]
-        for total in (ROWS_S, ROWS_A, ROWS_P):
-            scratch += [pltpu.VMEM((3, total >> k, LANES), BF) for k in range(5)]
-        scratch += [pltpu.SemaphoreType.DMA((12,)), pltpu.SemaphoreType.DMA((4,)),
-                    pltpu.SemaphoreType.DMA((3, 8, 3)), pltpu.SemaphoreType.DMA((3, 8, 3))]
-        dz_in, ds_in, fs, fa, fp = pl.pallas_call(
+        scratch += [pltpu.VMEM(shape, BF) for shape in finals[2:]]
+        scratch += [pltpu.VMEM((3, ROWS_A >> k, LANES), BF) for k in range(5)]
+        scratch += [pltpu.VMEM((3, ROWS_P, LANES), BF)] + [pltpu.VMEM((3, ROWS_P // 2, LANES), BF) for _ in range(4)]
+        scratch += [pltpu.SemaphoreType.DMA((12,)), pltpu.SemaphoreType.DMA((5,)), pltpu.SemaphoreType.DMA((toks // (8 * num_tok),)),
+                    pltpu.SemaphoreType.DMA((4,)), pltpu.SemaphoreType.DMA((5, 8, 3)), pltpu.SemaphoreType.DMA((5, 8, 3))]
+        packed = pl.pallas_call(
             body_kernel,
-            out_shape=[jax.ShapeDtypeStruct((toks, dim), BF), jax.ShapeDtypeStruct((rows, width), BF)] + [
-                jax.ShapeDtypeStruct((3, total, LANES), BF) for total in (ROWS_S, ROWS_A, ROWS_P)],
+            out_shape=[jax.ShapeDtypeStruct(shape, BF) for shape in finals],
             in_specs=[hbm] * 12 + [vmem] * 5,
-            out_specs=[vmem] * 5,
+            out_specs=[hbm] * 6,
             scratch_shapes=scratch,
             compiler_params=pltpu.CompilerParams(collective_id=0, has_side_effects=True, vmem_limit_bytes=60 * 2 ** 20),
             name="block",
         )(*big, *small)
-        shapes = [w_pa.shape, w_pb.shape, w_po.shape, w_bias.shape, w_q.shape, (1, width), w_kv.shape, w_g.shape, w_o.shape,
+        shapes = [w_pa.shape, w_pb.shape, w_po.shape, (HEADS, dim), w_q.shape, (width,), w_kv.shape, w_g.shape, w_o.shape,
                   w_sa.shape, w_sb.shape, w_so.shape]
-        grads = pl.pallas_call(
+        done = pl.pallas_call(
             unpack_kernel,
-            out_shape=[jax.ShapeDtypeStruct(shape, F32) for shape in shapes],
-            in_specs=[vmem] * 3,
-            out_specs=[hbm] * 12,
-            scratch_shapes=[pltpu.VMEM(shape, F32) for shape in shapes] + [pltpu.SemaphoreType.DMA((12,))],
-            compiler_params=pltpu.CompilerParams(vmem_limit_bytes=40 * 2 ** 20),
+            out_shape=[jax.ShapeDtypeStruct(shape, BF) for shape in finals[:2]] + [jax.ShapeDtypeStruct(shape, F32) for shape in shapes],
+            in_specs=[hbm] * 6,
+            out_specs=[hbm] * 14,
+            scratch_shapes=[pltpu.VMEM(shape, BF) for shape in finals] + [pltpu.VMEM(shape, F32) for shape in shapes] + [
+                pltpu.SemaphoreType.DMA((6,)), pltpu.SemaphoreType.DMA((14,))],
+            compiler_params=pltpu.CompilerParams(vmem_limit_bytes=56 * 2 ** 20),
             name="unpack",
-        )(fs, fa, fp)
-        grads = list(grads)
-        grads[5] = grads[5].reshape(width)
-        return (dz_in.reshape(pair_z.shape), ds_in.reshape(single_s.shape)) + tuple(grads)
+        )(*packed)
+        grads = list(done[2:])
+        grads[3] = grads[3].T
+        return (done[0].reshape(pair_z.shape), done[1].reshape(single_s.shape)) + tuple(grads)
 
     in_specs = (pair_spec, single_spec, P('dp', None), pair_spec, single_spec) + (P(),) * 12
     out_specs = (pair_spec, single_spec) + (P(),) * 12

time: 119 us -> 95.8 us (0.81)
  Pallas kernels: 108 us -> 95 us
  local copies, waits for them, and re-layouts: 9.56 us -> 0 us
    pallas_call x2, Pallas kernels: 108 us -> 95 us  [the longest x1 88 us: body(): pl.pallas_call(body_kernel, out_shape=[jax.ShapeDtypeStruct(shape, BF) fo...]
    unnamed x14 -> x0, local copies, waits for them, and re-layouts: 8.32 us -> none
    reshape x1 -> x0, local copies, waits for them, and re-layouts: 1.24 us -> none  [body(): q_bias.reshape(1, width)]
where the time goes in v2:
time: 95.8 us; the launch traced here: 95.6 us
  Pallas kernels  95 us (99%)
    pallas_call x1, Pallas kernels, body(): pl.pallas_call(body_kernel, out_shape=[jax.ShapeDtypeStruct(shape, BF) fo...  88 us
    pallas_call x1, Pallas kernels, body(): pl.pallas_call(unpack_kernel, out_shape=[jax.ShapeDtypeStruct(shape, BF)...  7 us

profile of v2, /device:TPU:0, one launch (start us, length us, event | category | flops | bytes accessed | tf_op | source)
XLA Modules:
  0.0 95.6 jit_solution(3665123905064227479)
XLA Ops:
  0.7 88.0 %block.1 = (bf16[6144,128]{1,0:T(8,128)(2,1)}, bf16[96,384]{1,0:T(8,128)(2,1)}, bf16[3,2,2,2,384,128]{5,4,3,2,1,0:T(8,128)(2,1)}, bf16[3,2,2,384,128]{4,3,2,1,0:...) custom-call(bf16[6144,128]{1,0:T(8,128)(2,1)} %bitcast.8, bf16[6144,128]{1,0:T(8,128)(2,1)} %bitcast.9, ...), custom_call_target="tpu_custom_call" | custom-call | tf_op jit(solution)/shard_map/block/pallas_call | solution.py:627
  88.6 7.0 %unpack.1 = (bf16[6144,128]{1,0:T(8,128)(2,1)}, bf16[96,384]{1,0:T(8,128)(2,1)}, f32[128,512]{1,0:T(8,128)}, f32[128,512]{1,0:T(8,128)}, f32[512,128]{1,0:T(8,12...) custom-call(bf16[6144,128]{1,0:T(8,128)(2,1)} %get-tuple-element.34., ...), custom_call_target="tpu_custom_call" | custom-call | tf_op jit(solution)/shard_map/unpack/pallas_call | solution.py:638

commit v3 on v2

--- a/solution.py
+++ b/solution.py
@@ -11,7 +11,7 @@
 MASK_BIG = 1e9
 BF = jnp.bfloat16
 F32 = jnp.float32
-ROWS_A, ROWS_P = 2048, 544
+ROWS_A, ROWS_K, ROWS_P = 1280, 768, 544
 LANES = 128
 
 
@@ -53,7 +53,7 @@
 
 AXES = ("x", "y", "z")
 ORDER = (("x", "y", "z"), ("y", "z", "x"), ("z", "x", "y"))
-ORDER_YZ = (("y", "z"), ("z", "y"), ("y", "z"))
+ORDER_XY = (("x", "y"), ("y", "x"), ("x", "y"))
 
 
 def remote(place, src, dst, send_sem, recv_sem, axis):
@@ -172,8 +172,8 @@
 
     def copy(self, core, stage, third):
         coords = self.place["coords"]
-        order = ORDER[third] if core == 0 else ORDER_YZ[third]
-        axes = AXES if core == 0 else AXES[1:]
+        order = ORDER[third] if core == 0 else ORDER_XY[third]
+        axes = AXES if core == 0 else AXES[:2]
         if stage > len(order):
             ref, axis, slot = self.bufs[core].at[third], "core", 4 + core
         else:
@@ -201,11 +201,12 @@
 def body_kernel(
         z_hbm, dz_hbm, wpa_hbm, wpb_hbm, wpo_hbm, wq_hbm, wkv_hbm, wg_hbm, wo_hbm, wsa_hbm, wsb_hbm, wso_hbm,
         s_ref, ds_ref, mask_ref, qb_ref, wbias_ref,
-        dzin_hbm, dsin_hbm, fs0_hbm, fs1_hbm, fa_hbm, fp_hbm,
+        dzin_hbm, dsin_hbm, fs0_hbm, fs1_hbm, fa_hbm, fk_hbm, fp_hbm,
         z_v, dz_v, wpa, wpb, wpo, wq, wkv, wg, wo, wsa, wsb, wso,
-        z1_v, w8, bias_v, prob_v, act_v, q_v, gate_v, att_v, gated_v, gatt_v, gmid_v, kv_v, gkv_v, gkvr_v,
-        dwpa, dwpb, dwpo, m8, dzin_ref, dsin_ref, c_all, ds_all, d_ab, d_so, fs0, fs1, fa_ref, fp_ref,
-        ga_, ga0, ga1, ga2, ga3, gp, gp0, gp1, gp2, gp3,
+        z1_v, w8, bias_v, prob_v, act_v, q_v, gate_v, att_v, gated_v, gatt_v, gmid_v, gact_v, kv_v, gkv_v, gkvr_v,
+        dwpa, dwpb, dwpo, m8, dzin_ref, dsin_ref, c_all, ds_all, d_ab, d_so, gnew_v, gab_v,
+        u0, u1, ut0, ut1, gn0, gn1, gnt0, gnt1, fs0, fs1, fa_ref, fk_ref, fp_ref,
+        ga_, ga0, ga1, ga2, ga3, gk, gk0, gk1, gk2, gk3, gp, gp0, gp1, gp2, gp3,
         in_sem, out_sem, dz_sem, kv_sem, send_sem, recv_sem):
     dap = lax.axis_index("dap")
     dp = lax.axis_index("dp")
@@ -232,20 +233,19 @@
     barrier = pltpu.get_barrier_semaphore()
     for peer in peers.values():
         pl.semaphore_signal(barrier, inc=1, device_id=peer, device_id_type=pl.DeviceIdType.MESH)
-    pl.semaphore_wait(barrier, 4)
 
     red_a = Reducer(place, ROWS_A, ga_, (ga0, ga1, ga2, ga3), fa_ref, send_sem.at[0], recv_sem.at[0])
     red_p = Doubler(place, ROWS_P, gp, (gp0, gp1, gp2, gp3), fp_ref, send_sem.at[1], recv_sem.at[1])
     gat_ds = Gatherer(place, ds_all, send_sem.at[2], recv_sem.at[2])
     gat_c = Gatherer(place, c_all, send_sem.at[3], recv_sem.at[3])
     tiles = Tiles(place, fs0, fs1, send_sem.at[4], recv_sem.at[4])
+    red_k = Reducer(place, ROWS_K, gk, (gk0, gk1, gk2, gk3), fk_ref, send_sem.at[5], recv_sem.at[5])
 
     def own_block(buf, value):
         for t in range(3):
             buf[t, core, cx, cy, dap] = value[:, t * LANES:(t + 1) * LANES]
 
     own_block(ds_all, ds_ref[...])
-    gat_ds.step(1)
 
     s_f = s_ref[...].astype(F32)
     s_norm, s_inv = layer_norm(s_f)
@@ -264,7 +264,9 @@
             src_ref=gkv_v.at[1 - dap], dst_ref=gkvr_v, send_sem=kv_sem.at[2], recv_sem=kv_sem.at[3],
             device_id=peers["z"], device_id_type=pl.DeviceIdType.MESH)
 
+    pl.semaphore_wait(barrier, 4)
     kv_copy().start()
+    gat_ds.step(1)
     copies[1].wait()
     copies[2].wait()
     q_v[...] = (nn(act, wq[...]) + qb_ref[...].astype(F32).reshape(1, width)).astype(BF)
@@ -288,30 +290,51 @@
     def side_by_side(tokens):
         return jnp.concatenate([tokens[k * num_tok:(k + 1) * num_tok] for k in range(8)], axis=1)
 
-    def pair_forward(b, carry):
-        at = pl.ds(pl.multiple_of(b * blk, blk), blk)
-        z_f = z_v[at, :].astype(F32)
-        normed, _ = layer_norm(z_f)
-        u = normed.astype(BF)
-        total = z_f
+    def rows_at(b):
+        return pl.ds(pl.multiple_of(b * blk, blk), blk)
+
+    def bias_at(b):
+        return b // per_cplx, pl.ds(pl.multiple_of(lax.rem(b, per_cplx) * 8, 8), 8)
+
+    def forward_norm(b, u_ref):
+        normed, _ = layer_norm(z_v[rows_at(b), :].astype(F32))
+        u_ref[...] = normed.astype(BF)
+
+    def forward_main(b, u_ref):
+        total = z_v[rows_at(b), :].astype(F32)
         for f in range(0, 512, 256):
+            u = u_ref[...]
             ha = nn(u, wpa[:, f:f + 256])
             hb = nn(u, wpb[:, f:f + 256])
             hidden = (ha * sigmoid(ha) * hb).astype(BF)
             total = total + nn(hidden, wpo[f:f + 256, :])
-        z1 = total.astype(BF)
-        z1_v[at, :] = z1
-        bias_norm, _ = layer_norm(z1.astype(F32))
-        bias8 = nt(w8[...], side_by_side(bias_norm.astype(BF)))
-        c, i0 = b // per_cplx, pl.multiple_of(lax.rem(b, per_cplx) * 8, 8)
-        bias_v[c, :, pl.ds(i0, 8), :] = bias8.reshape(HEADS, 8, num_tok)
-        for when, stage in ((2, 2), (5, 3), (9, 4)):
-            @pl.when(b == when)
+        z1_v[rows_at(b), :] = total.astype(BF)
+
+    def forward_bias(b):
+        bias_norm, _ = layer_norm(z1_v[rows_at(b), :].astype(F32))
+        c, at = bias_at(b)
+        bias_v[c, :, at, :] = nt(w8[...], side_by_side(bias_norm.astype(BF))).reshape(HEADS, 8, num_tok)
+
+    def forward_pair(p, carry):
+        forward_bias(2 * p)
+        forward_norm(2 * p + 2, u0)
+        forward_main(2 * p + 1, u1)
+        forward_bias(2 * p + 1)
+        forward_norm(2 * p + 3, u1)
+        forward_main(2 * p + 2, u0)
+        for when, stage in ((1, 2), (4, 3)):
+            @pl.when(p == when)
             def _():
                 gat_ds.step(stage)
         return carry
 
-    lax.fori_loop(0, num_blk, pair_forward, 0)
+    forward_norm(0, u0)
+    forward_norm(1, u1)
+    forward_main(0, u0)
+    lax.fori_loop(0, num_blk // 2 - 1, forward_pair, 0)
+    forward_bias(num_blk - 2)
+    forward_main(num_blk - 1, u1)
+    forward_bias(num_blk - 1)
 
     scale = HEAD_DIM ** -0.5
     grow = lax.broadcasted_iota(jnp.int32, (HEADS, 1, width), 0) * HEAD_DIM
@@ -346,7 +369,6 @@
     mid_act = mid_norm.astype(BF)
     own_block(c_all, mid_act)
     gat_c.step(1)
-    gat_ds.step(5)
 
     for k in range(8, 11):
         copies[k].wait()
@@ -368,17 +390,18 @@
     gatt_v[...] = (grad_gated * gate).astype(BF)
     grad_gate_pre = (grad_gated * att_v[...] * gate * (1.0 - gate)).astype(BF)
 
-    def put_attn(name_row, value):
+    def put_attn(buf, name_row, value):
         val = value.astype(BF)
+        per = val.shape[1] // width
         for k in range(val.shape[1] // LANES):
-            per = val.shape[1] // width
             lo = name_row + (k % per) * 384
-            ga_[k // per, lo:lo + 384, :] = val[:, k * LANES:(k + 1) * LANES]
-
+            buf[k // per, lo:lo + 384, :] = val[:, k * LANES:(k + 1) * LANES]
+
+    act_t = act_v[...].T
+    put_attn(ga_, 384, nn(act_t, grad_gate_pre))
+    put_attn(ga_, 768, tn(gated_v[...], grad_mid_bf))
     gat_c.step(2)
-    act_t = act_v[...].T
-    put_attn(1152, nn(act_t, grad_gate_pre))
-    put_attn(1536, tn(gated_v[...], grad_mid_bf))
+    gat_ds.step(4)
 
     grad_q_parts = []
     for c in range(num_cplx):
@@ -396,30 +419,31 @@
         for d in range(2):
             gkv_v[d, rows, 0:width] = grad_keys[d * half:(d + 1) * half].astype(BF)
             gkv_v[d, rows, width:2 * width] = grad_vals[d * half:(d + 1) * half].astype(BF)
-    gkv_copy().start()
     grad_q = jnp.concatenate(grad_q_parts, axis=0)
     grad_q_bf = grad_q.astype(BF)
-    put_attn(0, nn(act_t, grad_q_bf))
+    put_attn(ga_, 0, nn(act_t, grad_q_bf))
     row16 = lax.broadcasted_iota(jnp.int32, (16, width), 0)
     bias_tile = jnp.where(row16 == 0, jnp.sum(grad_q, axis=0, keepdims=True), 0.0).astype(BF)
     for t in range(3):
-        ga_[t, 1920:1936, :] = bias_tile[:, t * LANES:(t + 1) * LANES]
-        ga_[t, 1936:2048, :] = jnp.zeros((112, LANES), BF)
-    grad_act = nt(grad_q_bf, wq[...]) + nt(grad_gate_pre, wg[...])
-    gkv_copy().wait()
-    grad_kv = (gkv_v[dap].astype(F32) + gkvr_v[...].astype(F32)).astype(BF)
-    put_attn(384, nn(act_t, grad_kv))
+        ga_[t, 1152:1168, :] = bias_tile[:, t * LANES:(t + 1) * LANES]
+        ga_[t, 1168:1280, :] = jnp.zeros((112, LANES), BF)
     red_a.start()
-    gat_c.step(3)
-    grad_act = grad_act + nt(grad_kv, wkv[...])
-    s_norm2, s_inv2 = layer_norm(s_ref[...].astype(F32))
-    dsin_ref[...] = (gmid_v[...] + norm_grad(s_norm2, s_inv2, grad_act)).astype(BF)
-    outs = [(dsin_ref, dsin_hbm), (fs0, fs0_hbm), (fs1, fs1_hbm), (fa_ref, fa_hbm), (fp_ref, fp_hbm)]
+    gact_v[...] = nt(grad_q_bf, wq[...]) + nt(grad_gate_pre, wg[...])
+
+    def finish_attention():
+        gkv_copy().wait()
+        grad_kv = (gkv_v[dap].astype(F32) + gkvr_v[...].astype(F32)).astype(BF)
+        put_attn(gk, 0, tn(act_v[...], grad_kv))
+        red_k.start()
+        grad_act = gact_v[...] + nt(grad_kv, wkv[...])
+        s_norm2, s_inv2 = layer_norm(s_ref[...].astype(F32))
+        dsin_ref[...] = (gmid_v[...] + norm_grad(s_norm2, s_inv2, grad_act)).astype(BF)
+
+    outs = [(dsin_ref, dsin_hbm), (fs0, fs0_hbm), (fs1, fs1_hbm), (fa_ref, fa_hbm), (fk_ref, fk_hbm), (fp_ref, fp_hbm)]
     out_copies = [pltpu.make_async_copy(src, dst, out_sem.at[k]) for k, (src, dst) in enumerate(outs)]
-    out_copies[0].start()
 
     def tile_grads():
-        tile = jnp.where(core == 0, 3 * (2 * cy + dap) + 2 * cx, 3 * (2 * cy + dap) + 1)
+        tile = jnp.where(core == 0, 3 * (2 * cx + cy) + 2 * dap, 3 * (2 * cx + cy) + 1)
         at = pl.ds(pl.multiple_of(tile * LANES, LANES), LANES)
         w_ab = jnp.concatenate([wsa[:, at], wsb[:, at]], axis=1)
         w_o_tile = wso[at, :]
@@ -441,7 +465,7 @@
         for k in range(2):
             @pl.when(core == k)
             def _():
-                slot = (cx, cy, dap) if k == 0 else (cy, dap)
+                slot = (cx, cy, dap) if k == 0 else (cx, cy)
                 buf = fs0 if k == 0 else fs1
                 buf[(0,) + slot] = d_ab[:, :LANES].astype(BF)
                 buf[(1,) + slot] = d_ab[:, LANES:].astype(BF)
@@ -463,48 +487,78 @@
         return pltpu.make_async_copy(dzin_ref.at[at, :], dzin_hbm.at[at, :], dz_sem.at[k])
 
     hooks = {
-        0: hook(lambda: red_a.step(1)),
-        2: hook(lambda: gat_c.step(4), lambda: red_a.step(2)),
-        3: hook(lambda: gat_c.step(5), tile_grads, lambda: tiles.step(1)),
-        4: hook(lambda: red_a.step(3)),
-        5: hook(lambda: tiles.step(2)),
-        6: hook(lambda: red_a.step(4)),
+        0: hook(lambda: gat_c.step(3), lambda: gkv_copy().start()),
+        1: hook(lambda: red_a.step(1)),
+        2: hook(lambda: gat_c.step(4)),
+        3: hook(lambda: gat_c.step(5), lambda: gat_ds.step(5), tile_grads, lambda: tiles.step(1), lambda: red_a.step(2)),
+        4: hook(finish_attention, lambda: red_a.step(3)),
+        5: hook(lambda: tiles.step(2), lambda: red_a.step(4), lambda: red_k.step(1)),
+    }
+    tail_hooks = {
+        2: hook(lambda: red_p.step(1)),
+        4: hook(lambda: red_k.step(2), lambda: red_a.step(5)),
         7: hook(lambda: tiles.step(3)),
-        8: hook(lambda: red_a.step(5)),
-        10: hook(lambda: red_a.step(6)),
-        11: hook(lambda: tiles.step(4)),
+        9: hook(lambda: red_p.step(2)),
+        11: hook(lambda: red_k.step(3), lambda: red_a.step(6)),
     }
 
-    def pair_backward(b, carry):
-        at = pl.ds(pl.multiple_of(b * blk, blk), blk)
-        c, i0 = b // per_cplx, pl.multiple_of(lax.rem(b, per_cplx) * 8, 8)
-        gl = bias_v[c, :, pl.ds(i0, 8), :].reshape(8 * HEADS, num_tok).astype(BF)
-        wide = tn(gl, w8[...])
+    def backward_head(b, live, bufs):
+        u_ref, ut_ref, gn_ref, gnt_ref = bufs
+        at = rows_at(b)
+        c, rows = bias_at(b)
+        gl_f = bias_v[c, :, rows, :].reshape(8 * HEADS, num_tok)
+        wide = tn(gl_f.astype(BF), w8[...])
         grad_norm = jnp.concatenate([wide[:, k * LANES:(k + 1) * LANES] for k in range(8)], axis=0)
         bias_norm, bias_inv = layer_norm(z1_v[at, :].astype(F32))
-        m8[...] += nn(gl, side_by_side(bias_norm.astype(BF)))
+        m8[...] += nn((gl_f * live).astype(BF), side_by_side(bias_norm.astype(BF)))
         grad_new = dz_v[at, :].astype(F32) + norm_grad(bias_norm, bias_inv, grad_norm)
+        gnew_v[at, :] = grad_new
         gnb = grad_new.astype(BF)
-        gnb_t = gnb.T
-        normed, inv = layer_norm(z_v[at, :].astype(F32))
+        gn_ref[...] = gnb
+        gnt_ref[...] = gnb.T
+        normed, _ = layer_norm(z_v[at, :].astype(F32))
         u = normed.astype(BF)
-        u_t = u.T
-        grad_normed = None
+        u_ref[...] = u
+        ut_ref[...] = u.T
+
+    def backward_main(b, bufs):
+        u_ref, ut_ref, gn_ref, gnt_ref = bufs
+        at = rows_at(b)
         for f in range(0, 512, 256):
             cols = slice(f, f + 256)
+            u, gnb = u_ref[...], gn_ref[...]
             hidden, grad_a, grad_b = swiglu_grad(nn(u, wpa[:, cols]), nn(u, wpb[:, cols]), nt(gnb, wpo[cols, :]))
-            dwpo[:, cols] += nn(gnb_t, hidden)
-            dwpa[:, cols] += nn(u_t, grad_a)
-            dwpb[:, cols] += nn(u_t, grad_b)
-            part = nt(grad_a, wpa[:, cols]) + nt(grad_b, wpb[:, cols])
-            grad_normed = part if grad_normed is None else grad_normed + part
-        dzin_ref[at, :] = (grad_new + norm_grad(normed, inv, grad_normed)).astype(BF)
+            gab_v[at, cols] = grad_a
+            gab_v[at, 512 + f:768 + f] = grad_b
+            dwpo[:, cols] += nn(gnt_ref[...], hidden)
+            dwpa[:, cols] += nn(ut_ref[...], grad_a)
+            dwpb[:, cols] += nn(ut_ref[...], grad_b)
+
+    def backward_tail(b, carry):
+        at = rows_at(b)
+        grad_normed = nt(gab_v[at, :], jnp.concatenate([wpa[...], wpb[...]], axis=1))
+        normed, inv = layer_norm(z_v[at, :].astype(F32))
+        dzin_ref[at, :] = (gnew_v[at, :] + norm_grad(normed, inv, grad_normed)).astype(BF)
         dz_copy(b).start()
-        for when, todo in hooks.items():
+        for when, todo in tail_hooks.items():
             pl.when(b == when)(todo)
         return carry
 
-    lax.fori_loop(0, num_blk, pair_backward, 0)
+    bufs0, bufs1 = (u0, ut0, gn0, gnt0), (u1, ut1, gn1, gnt1)
+
+    def backward_pair(p, carry):
+        backward_head(2 * p + 1, 1.0, bufs1)
+        backward_main(2 * p, bufs0)
+        more = jnp.where(p < num_blk // 2 - 1, 1.0, 0.0)
+        backward_head(jnp.minimum(2 * p + 2, num_blk - 1), more, bufs0)
+        backward_main(2 * p + 1, bufs1)
+        for when, todo in hooks.items():
+            pl.when(p == when)(todo)
+        return carry
+
+    backward_head(0, 1.0, bufs0)
+    lax.fori_loop(0, num_blk // 2, backward_pair, 0)
+    out_copies[0].start()
 
     for t, ref in enumerate((dwpa, dwpb, dwpo)):
         for k in range(4):
@@ -517,17 +571,23 @@
     for t in range(1, 3):
         gp[t, 512:528, :] = jnp.zeros((16, LANES), BF)
     red_p.start()
-    red_p.step(1)
+    lax.fori_loop(0, num_blk, backward_tail, 0)
+    red_p.step(3)
+    red_k.step(4)
     red_a.step(7)
-    red_p.step(2)
+    red_k.step(5)
+    red_p.step(4)
+    tiles.step(4)
+    red_a.step(8)
+    out_copies[3].start()
+    red_k.step(6)
+    red_p.step(5)
+    out_copies[5].start()
+    red_k.step(7)
     tiles.step(5)
     out_copies[1].start()
     out_copies[2].start()
-    red_a.step(8)
-    out_copies[3].start()
-    red_p.step(3)
-    red_p.step(4)
-    red_p.step(5)
+    red_k.step(8)
     out_copies[4].start()
 
     def drain(k, carry):
@@ -539,10 +599,10 @@
         item.wait()
 
 
-def unpack_kernel(dz_i, ds_i, fs0_i, fs1_i, fa_i, fp_i,
+def unpack_kernel(dz_i, ds_i, fs0_i, fs1_i, fa_i, fk_i, fp_i,
                   dz_o, ds_o, pa_o, pb_o, po_o, bias_o, q_o, qb_o, kv_o, g_o, o_o, sa_o, sb_o, so_o,
-                  dz, ds, fs0, fs1, fa, fp, pa, pb, po, bias, q, qb, kv, g, o, sa, sb, so, in_sem, sem):
-    ins = [(fs0_i, fs0), (fs1_i, fs1), (fa_i, fa), (fp_i, fp), (dz_i, dz), (ds_i, ds)]
+                  dz, ds, fs0, fs1, fa, fk, fp, pa, pb, po, bias, q, qb, kv, g, o, sa, sb, so, in_sem, sem):
+    ins = [(fs0_i, fs0), (fs1_i, fs1), (fa_i, fa), (fp_i, fp), (dz_i, dz), (ds_i, ds), (fk_i, fk)]
     reads = [pltpu.make_async_copy(src, dst, in_sem.at[k]) for k, (src, dst) in enumerate(ins)]
     for item in reads:
         item.start()
@@ -554,10 +614,10 @@
     reads[1].wait()
     for kind in range(3):
         for pair in range(4):
-            cy, cz = pair // 2, pair % 2
+            cx, cy = pair // 2, pair % 2
             for j in range(3):
                 lo = (3 * pair + j) * LANES
-                tile = fs1[kind, cy, cz] if j == 1 else fs0[kind, j // 2, cy, cz]
+                tile = fs1[kind, cx, cy] if j == 1 else fs0[kind, cx, cy, j // 2]
                 wide = tile.astype(F32)
                 if kind < 2:
                     (sa, sb)[kind][:, lo:lo + LANES] = wide
@@ -566,14 +626,15 @@
                         so[lo:lo + LANES, k * LANES:(k + 1) * LANES] = wide[k * LANES:(k + 1) * LANES]
         copies[kind].start()
     reads[2].wait()
-    for index, (ref, row) in enumerate(((q, 0), (kv, 384), (g, 1152), (o, 1536))):
+    reads[6].wait()
+    for index, (ref, buf, row) in enumerate(((q, fa, 0), (kv, fk, 0), (g, fa, 384), (o, fa, 768))):
         per = ref.shape[1] // 384
         for k in range(3 * per):
             lo = row + (k % per) * 384
-            ref[:, k * LANES:(k + 1) * LANES] = fa[k // per, lo:lo + 384, :].astype(F32)
+            ref[:, k * LANES:(k + 1) * LANES] = buf[k // per, lo:lo + 384, :].astype(F32)
         copies[3 + index].start()
     for t in range(3):
-        qb[t * LANES:(t + 1) * LANES] = fa[t, 1920:1936, :].astype(F32)[0]
+        qb[t * LANES:(t + 1) * LANES] = fa[t, 1152:1168, :].astype(F32)[0]
     copies[7].start()
     reads[3].wait()
     for t, ref in enumerate((pa, pb)):
@@ -606,29 +667,33 @@
         big = (pair_z.reshape(toks, dim), dz_out.reshape(toks, dim), w_pa, w_pb, w_po, w_q, w_kv, w_g, w_o, w_sa, w_sb, w_so)
         small = (single_s.reshape(rows, width), ds_out.reshape(rows, width), token_mask, q_bias, w_bias.T)
         scratch = [pltpu.VMEM(a.shape, a.dtype) for a in big]
-        finals = [(toks, dim), (rows, width), (3, 2, 2, 2, width, LANES), (3, 2, 2, width, LANES), (3, ROWS_A, LANES), (3, ROWS_P, LANES)]
+        finals = [(toks, dim), (rows, width), (3, 2, 2, 2, width, LANES), (3, 2, 2, width, LANES), (3, ROWS_A, LANES), (3, ROWS_K, LANES), (3, ROWS_P, LANES)]
         scratch += [
             pltpu.VMEM((toks, dim), BF), pltpu.VMEM((128, 1024), BF),
             pltpu.VMEM((num_cplx, HEADS, half, num_tok), F32), pltpu.VMEM((num_cplx, HEADS * half, num_tok), F32),
             pltpu.VMEM((rows, width), BF), pltpu.VMEM((rows, width), BF), pltpu.VMEM((rows, width), F32),
             pltpu.VMEM((rows, width), F32), pltpu.VMEM((rows, width), BF), pltpu.VMEM((rows, width), BF),
-            pltpu.VMEM((rows, width), F32),
+            pltpu.VMEM((rows, width), F32), pltpu.VMEM((rows, width), F32),
             pltpu.VMEM((2, rows, 2 * width), BF), pltpu.VMEM((2, rows, 2 * width), BF), pltpu.VMEM((rows, 2 * width), BF),
             pltpu.VMEM((128, 512), F32), pltpu.VMEM((128, 512), F32), pltpu.VMEM((128, 512), F32), pltpu.VMEM((128, 1024), F32),
             pltpu.VMEM(finals[0], BF), pltpu.VMEM(finals[1], BF),
             pltpu.VMEM((3, 2, 2, 2, 2, rows, LANES), BF), pltpu.VMEM((3, 2, 2, 2, 2, rows, LANES), BF),
             pltpu.VMEM((width, 2 * LANES), F32), pltpu.VMEM((LANES, width), F32),
+            pltpu.VMEM((toks, dim), F32), pltpu.VMEM((toks, 1024), BF),
         ]
+        for _ in range(2):
+            scratch += [pltpu.VMEM((512, dim), BF)] * 2 + [pltpu.VMEM((dim, 512), BF)] * 2
         scratch += [pltpu.VMEM(shape, BF) for shape in finals[2:]]
-        scratch += [pltpu.VMEM((3, ROWS_A >> k, LANES), BF) for k in range(5)]
+        for total in (ROWS_A, ROWS_K):
+            scratch += [pltpu.VMEM((3, total >> k, LANES), BF) for k in range(5)]
         scratch += [pltpu.VMEM((3, ROWS_P, LANES), BF)] + [pltpu.VMEM((3, ROWS_P // 2, LANES), BF) for _ in range(4)]
-        scratch += [pltpu.SemaphoreType.DMA((12,)), pltpu.SemaphoreType.DMA((5,)), pltpu.SemaphoreType.DMA((toks // (8 * num_tok),)),
-                    pltpu.SemaphoreType.DMA((4,)), pltpu.SemaphoreType.DMA((5, 8, 3)), pltpu.SemaphoreType.DMA((5, 8, 3))]
+        scratch += [pltpu.SemaphoreType.DMA((12,)), pltpu.SemaphoreType.DMA((6,)), pltpu.SemaphoreType.DMA((toks // (8 * num_tok),)),
+                    pltpu.SemaphoreType.DMA((4,)), pltpu.SemaphoreType.DMA((6, 8, 3)), pltpu.SemaphoreType.DMA((6, 8, 3))]
         packed = pl.pallas_call(
             body_kernel,
             out_shape=[jax.ShapeDtypeStruct(shape, BF) for shape in finals],
             in_specs=[hbm] * 12 + [vmem] * 5,
-            out_specs=[hbm] * 6,
+            out_specs=[hbm] * 7,
             scratch_shapes=scratch,
             compiler_params=pltpu.CompilerParams(collective_id=0, has_side_effects=True, vmem_limit_bytes=60 * 2 ** 20),
             name="block",
@@ -638,10 +703,10 @@
         done = pl.pallas_call(
             unpack_kernel,
             out_shape=[jax.ShapeDtypeStruct(shape, BF) for shape in finals[:2]] + [jax.ShapeDtypeStruct(shape, F32) for shape in shapes],
-            in_specs=[hbm] * 6,
+            in_specs=[hbm] * 7,
             out_specs=[hbm] * 14,
             scratch_shapes=[pltpu.VMEM(shape, BF) for shape in finals] + [pltpu.VMEM(shape, F32) for shape in shapes] + [
-                pltpu.SemaphoreType.DMA((6,)), pltpu.SemaphoreType.DMA((14,))],
+                pltpu.SemaphoreType.DMA((7,)), pltpu.SemaphoreType.DMA((14,))],
             compiler_params=pltpu.CompilerParams(vmem_limit_bytes=56 * 2 ** 20),
             name="unpack",
         )(*packed)

time: 95.8 us -> 91 us (0.950)
  Pallas kernels: 95 us -> 90 us
    pallas_call x1, Pallas kernels: 88 us -> 83 us  [body(): pl.pallas_call(body_kernel, out_shape=[jax.ShapeDtypeStruct(shape, BF) fo...]
where the time goes in v3:
time: 91 us; the launch traced here: 90.9 us
  Pallas kernels  90 us (99%)
    pallas_call x1, Pallas kernels, body(): pl.pallas_call(body_kernel, out_shape=[jax.ShapeDtypeStruct(shape, BF) fo...  83 us
    pallas_call x1, Pallas kernels, body(): pl.pallas_call(unpack_kernel, out_shape=[jax.ShapeDtypeStruct(shape, BF)...  7.01 us

profile of v3, /device:TPU:0, one launch (start us, length us, event | category | flops | bytes accessed | tf_op | source)
XLA Modules:
  0.0 90.9 jit_solution(3306005362720447281)
XLA Ops:
  0.7 83.0 %block.1 = (bf16[6144,128]{1,0:T(8,128)(2,1)}, bf16[96,384]{1,0:T(8,128)(2,1)}, bf16[3,2,2,2,384,128]{5,4,3,2,1,0:T(8,128)(2,1)}, bf16[3,2,2,384,128]{4,3,2,1,0:...) custom-call(bf16[6144,128]{1,0:T(8,128)(2,1)} %bitcast.8, ...), custom_call_target="tpu_custom_call" | custom-call | tf_op jit(solution)/shard_map/block/pallas_call | solution.py:692
  83.7 7.0 %unpack.1 = (bf16[6144,128]{1,0:T(8,128)(2,1)}, bf16[96,384]{1,0:T(8,128)(2,1)}, f32[128,512]{1,0:T(8,128)}, f32[128,512]{1,0:T(8,128)}, f32[512,128]{1,0:T(8,12...) custom-call(bf16[6144,128]{1,0:T(8,128)(2,1)} %get-tuple-element.35., ...), custom_call_target="tpu_custom_call" | custom-call | tf_op jit(solution)/shard_map/unpack/pallas_call | solution.py:703
